TPU v7x, 32 devices: a whole 2x2x4 slice. The times are simulated.
32 devices in a mesh: groups: 2 (over y), inner: 4 (over z), outer: 2 (over x), head: 2 (over core).
Axes of the slice: x: 2, y: 2, z: 4, core: 2. Of those that a mesh axis runs over, the one named last changes fastest.
Arguments:
- queries: bfloat16 [4, 512, 8, 128], P(('groups', 'outer'), 'inner', 'head'), parts along dimension 0, may hold values from -112 to 112
- keys: bfloat16 [4, 512, 128], P(('groups', 'outer'), 'inner'), parts along dimension 0, may hold values from -4 to 4
- values: bfloat16 [4, 512, 128], P(('groups', 'outer'), 'inner'), parts along dimension 0, may hold values from -6 to 6
- out: bfloat16 [4, 512, 8, 128], P(('groups', 'outer'), 'inner', 'head'), parts along dimension 0, may hold values from -6 to 6, as said below
- log_total: float32 [4, 8, 512], P(('groups', 'outer'), 'head', 'inner'), parts along dimension 0, as said below
- d_out: bfloat16 [4, 512, 8, 128], P(('groups', 'outer'), 'inner', 'head'), parts along dimension 0, may hold values from -6 to 6
- span_order: int32 [4, 8], P(('groups', 'outer')), parts along dimension 0, may hold values from 0 to 7, as said below
Outputs:
- grad_queries: bfloat16 [4, 512, 8, 128], P(('groups', 'outer'), 'inner', 'head'), parts along dimension 0
- grad_keys: bfloat16 [4, 512, 128], P(('groups', 'outer'), 'inner'), parts along dimension 0
- grad_values: bfloat16 [4, 512, 128], P(('groups', 'outer'), 'inner'), parts along dimension 0
There are 2 independent parts, one for each index of `groups`. A program takes and returns all parts, laid end to end along the dimension named above; each array names one. Nothing has to cross between parts.
Inputs may be any that keep to these rules, and one draw needn't show every extreme that they name: `span_order`: each row is a permutation of 0 to 7. `out`: the causal softmax attention output of queries, keys and values in the order given by span_order, rounded to bfloat16. `log_total`: the log of the causal softmax total of each query row and head for the same inputs.
All inputs are finite; a program needn't handle non-finite values.
Results may differ from a plain program's by a relative error of at most 0.0054.
Values may be sent and summed in bfloat16 or wider, within the bound.
A program may use at most 64 MiB of HBM per device.

v0:
```python
import functools
import math

import jax
import jax.numpy as jnp
from jax import lax
from jax.experimental import pallas as pl
from jax.experimental.pallas import tpu as pltpu
from jax.sharding import PartitionSpec as P

MESH = pl.DeviceIdType.MESH
F32 = jnp.float32
BF16 = jnp.bfloat16
NT = (((1,), (1,)), ((), ()))
TN = (((0,), (0,)), ((), ()))
LOG2E = math.log2(math.e)


def dot(a, b, dims=(((1,), (0,)), ((), ()))):
    return lax.dot_general(a, b, dims, preferred_element_type=F32)


def kernel(
    n,
    heads,
    q_hbm,
    k_hbm,
    v_hbm,
    o_hbm,
    l_hbm,
    g_hbm,
    order_hbm,
    dq_ref,
    kv_ref,
    qs,
    gs,
    os_,
    ls,
    kv,
    stat,
    ds_all,
    part,
    send_buf,
    recv_buf,
    dq_send,
    dq_recv,
    fin,
    order,
    load_sem,
    pair_send,
    pair_recv,
    kv_send,
    kv_recv,
    grad_send,
    grad_recv,
):
    me = lax.axis_index("inner")
    core = lax.axis_index("head")
    other = 1 - core
    half, width = kv.shape[2], kv.shape[3]
    rows = qs.shape[1]
    scale = 1.0 / math.sqrt(width)
    partner = {"head": other}

    def at(d):
        return {"inner": lax.rem(me + d, n)}

    barrier = pltpu.get_barrier_semaphore()
    near = sorted(range(1, n), key=lambda d: (-min(d, n - d), d))
    for d in near:
        pl.semaphore_signal(barrier, inc=1, device_id=at(d), device_id_type=MESH)
    pl.semaphore_signal(barrier, inc=1, device_id=partner, device_id_type=MESH)

    mine = pl.ds(pl.multiple_of(core * half, half), half)
    theirs = pl.ds(pl.multiple_of(other * half, half), half)
    loads = [
        pltpu.make_async_copy(src, dst, load_sem.at[i])
        for i, (src, dst) in enumerate(
            (
                (k_hbm.at[mine], kv.at[0, 0]),
                (v_hbm.at[mine], kv.at[0, 1]),
                (q_hbm, qs.at[0]),
                (g_hbm, gs.at[0]),
                (o_hbm, os_.at[0]),
                (l_hbm, ls.at[0]),
                (order_hbm, order),
            )
        )
    ]
    for load in loads:
        load.start()

    loads[0].wait()
    loads[1].wait()
    pl.semaphore_wait(barrier, n)
    kv_copies = {}
    for d in near:
        kv_copies[d] = pltpu.make_async_remote_copy(
            src_ref=kv.at[0],
            dst_ref=kv.at[d],
            send_sem=kv_send.at[d],
            recv_sem=kv_recv.at[d],
            device_id=at(d),
            device_id_type=MESH,
        )
        kv_copies[d].start()
    pair_copies = []
    for i, ref in enumerate((qs, gs, os_, ls)):
        loads[2 + i].wait()
        copy = pltpu.make_async_remote_copy(
            src_ref=ref.at[0],
            dst_ref=ref.at[1],
            send_sem=pair_send.at[i],
            recv_sem=pair_recv.at[i],
            device_id=partner,
            device_id_type=MESH,
        )
        copy.start()
        pair_copies.append(copy)

    toks = rows // heads
    col = lax.broadcasted_iota(jnp.int32, (toks, rows), 1)
    spread = jnp.where(
        col // heads == lax.broadcasted_iota(jnp.int32, (toks, rows), 0), 1.0, 0.0
    )
    head_of = lax.broadcasted_iota(jnp.int32, (heads, rows), 1) % heads
    pick = head_of == lax.broadcasted_iota(jnp.int32, (heads, rows), 0)
    ones = jnp.ones((8, width), BF16)

    def stats(i):
        total = jnp.dot(
            ls[i], spread, preferred_element_type=F32, precision=lax.Precision.HIGHEST
        )
        total = jnp.sum(jnp.where(pick, total, 0.0), axis=0, keepdims=True)
        prod = os_[i].astype(F32) * gs[i].astype(F32)
        high = prod.astype(BF16)
        low = (prod - high.astype(F32)).astype(BF16)
        delta = dot(ones, high, NT) + dot(ones, low, NT)
        stat[0:1, i * rows : (i + 1) * rows] = total * LOG2E
        stat[1:2, i * rows : (i + 1) * rows] = delta[0:1]

    stats(0)
    for copy in pair_copies:
        copy.wait_recv()
    stats(1)

    loads[6].wait()
    tok = (lax.broadcasted_iota(jnp.int32, (1, rows), 1)) // heads
    span = jnp.where(tok < half, order[2 * me], order[2 * me + 1])
    q_pos = span * half + tok % half
    q_pos = jnp.concatenate([q_pos, q_pos], axis=1)
    key_row = lax.broadcasted_iota(jnp.int32, (half, 1), 0)

    def block(d):
        owner = lax.rem(me + (n - d), n)
        k_pos = order[2 * owner + core] * half + key_row
        visible = k_pos <= q_pos
        queries = qs[...].reshape(2 * rows, width)
        grads = gs[...].reshape(2 * rows, width)
        scores = dot(kv[d, 0], queries, NT)
        grad_probs = dot(kv[d, 1], grads, NT)
        probs = jnp.exp2(
            jnp.where(visible, scores * (scale * LOG2E) - stat[0:1, :], -jnp.inf)
        )
        grad_scores = (probs * (grad_probs - stat[1:2, :]) * scale).astype(BF16)
        ds_all[d] = grad_scores
        yield 1, dot(probs.astype(BF16), grads)
        yield 0, dot(grad_scores, queries)

    for i, grad in block(0):
        part[i] = grad
    grad_copies = {}
    for d in reversed(near):
        kv_copies[d].wait_recv()
        for i, grad in block(d):
            send_buf[d, i] = grad.astype(BF16)
            grad_copies[d, i] = pltpu.make_async_remote_copy(
                src_ref=send_buf.at[d, i],
                dst_ref=recv_buf.at[d, i],
                send_sem=grad_send.at[d, i],
                recv_sem=grad_recv.at[d, i],
                device_id=at(n - d),
                device_id_type=MESH,
            )
            grad_copies[d, i].start()

    def query_grad(i):
        total = None
        for d in range(n):
            term = dot(ds_all[d, :, i * rows : (i + 1) * rows], kv[d, 0], TN)
            total = term if total is None else total + term
        return total

    dq_send[...] = query_grad(1)
    dq_copy = pltpu.make_async_remote_copy(
        src_ref=dq_send,
        dst_ref=dq_recv,
        send_sem=pair_send.at[4],
        recv_sem=pair_recv.at[4],
        device_id=partner,
        device_id_type=MESH,
    )
    dq_copy.start()
    own_grad = query_grad(0)
    dq_copy.wait_recv()
    dq_ref[...] = (own_grad + dq_recv[...]).astype(BF16)

    fin_copies = []
    for i in (1, 0):
        total = part[i]
        for d in reversed(near):
            grad_copies[d, i].wait_recv()
            total = total + recv_buf[d, i].astype(F32)
        fin[0, i] = total.astype(BF16)
        copy = pltpu.make_async_remote_copy(
            src_ref=fin.at[0, i],
            dst_ref=fin.at[1, i],
            send_sem=pair_send.at[5 + i],
            recv_sem=pair_recv.at[5 + i],
            device_id=partner,
            device_id_type=MESH,
        )
        copy.start()
        fin_copies.append(copy)
    kv_ref[:, mine] = fin[0]
    for copy in fin_copies:
        copy.wait_recv()
    kv_ref[:, theirs] = fin[1]
    for d in near:
        kv_copies[d].wait_send()
        grad_copies[d, 0].wait_send()
        grad_copies[d, 1].wait_send()
    for copy in pair_copies + [dq_copy] + fin_copies:
        copy.wait_send()


def store_kernel(dq_ref, kv_ref, dq_hbm, dk_hbm, dv_hbm, sem):
    pairs = ((dq_ref, dq_hbm), (kv_ref.at[0], dk_hbm), (kv_ref.at[1], dv_hbm))
    copies = [pltpu.make_async_copy(a, b, sem.at[i]) for i, (a, b) in enumerate(pairs)]
    for copy in copies:
        copy.start()
    for copy in copies:
        copy.wait()


def body(n, queries, keys, values, out, log_total, d_out, span_order):
    _, toks, heads, width = queries.shape
    rows = toks * heads
    half = toks // 2
    flat = lambda x: x.reshape(rows, width)
    anywhere = pl.BlockSpec(memory_space=pltpu.HBM)
    in_vmem = pl.BlockSpec(memory_space=pltpu.VMEM)
    dq, dkv = pl.pallas_call(
        functools.partial(kernel, n, heads),
        out_shape=(
            pltpu.VMEM((rows, width), BF16),
            pltpu.VMEM((2, toks, width), BF16),
        ),
        in_specs=[anywhere] * 7,
        out_specs=(in_vmem,) * 2,
        scratch_shapes=[
            pltpu.VMEM((2, rows, width), BF16),
            pltpu.VMEM((2, rows, width), BF16),
            pltpu.VMEM((2, rows, width), BF16),
            pltpu.VMEM((2, heads, toks), F32),
            pltpu.VMEM((n, 2, half, width), BF16),
            pltpu.VMEM((8, 2 * rows), F32),
            pltpu.VMEM((n, half, 2 * rows), BF16),
            pltpu.VMEM((2, half, width), F32),
            pltpu.VMEM((n, 2, half, width), BF16),
            pltpu.VMEM((n, 2, half, width), BF16),
            pltpu.VMEM((rows, width), F32),
            pltpu.VMEM((rows, width), F32),
            pltpu.VMEM((2, 2, half, width), BF16),
            pltpu.SMEM((span_order.shape[1],), jnp.int32),
            pltpu.SemaphoreType.DMA((7,)),
            pltpu.SemaphoreType.DMA((7,)),
            pltpu.SemaphoreType.DMA((7,)),
            pltpu.SemaphoreType.DMA((n,)),
            pltpu.SemaphoreType.DMA((n,)),
            pltpu.SemaphoreType.DMA((n, 2)),
            pltpu.SemaphoreType.DMA((n, 2)),
        ],
        compiler_params=pltpu.CompilerParams(collective_id=0, has_side_effects=True),
    )(
        flat(queries),
        keys[0],
        values[0],
        flat(out),
        log_total[0],
        flat(d_out),
        span_order[0],
    )
    dq, dk, dv = pl.pallas_call(
        store_kernel,
        out_shape=(
            jax.ShapeDtypeStruct((rows, width), BF16),
            jax.ShapeDtypeStruct((toks, width), BF16),
            jax.ShapeDtypeStruct((toks, width), BF16),
        ),
        in_specs=[in_vmem] * 2,
        out_specs=(anywhere,) * 3,
        scratch_shapes=[pltpu.SemaphoreType.DMA((3,))],
        compiler_params=pltpu.CompilerParams(vmem_limit_bytes=2**20),
    )(dq, dkv)
    return dq.reshape(queries.shape), dk[None], dv[None]


def solution(mesh):
    seq = ("groups", "outer")
    wide = P(seq, "inner", "head", None)
    narrow = P(seq, "inner", None)
    return jax.shard_map(
        functools.partial(body, mesh.shape["inner"]),
        mesh=mesh,
        in_specs=(wide, narrow, narrow, wide, P(seq, "head", "inner"), wide, P(seq, None)),
        out_specs=(wide, narrow, narrow),
        check_vma=False,
    )
```

profile of v0, /device:TPU:0, one launch (start us, length us, event | category | flops | bytes accessed | tf_op | source)
XLA Modules:
  0.0 16.5 jit_solution(1634863334346200752)
XLA Ops:
  0.6 15.1 %shard_map.94 = (bf16[512,128]{1,0:T(8,128)(2,1)S(1)}, bf16[2,128,128]{2,1,0:T(8,128)(2,1)S(1)}) custom-call(bf16[512,128]{1,0:T(8,128)(2,1)} %bitcast.10, bf16[128,128]{1,0:T(8,128)(2,1)} %bitcast.13, bf16[128,128]{1,0:T(8,128)(2,1)} %bitcast.14, bf16[512,128]{1,0:T(8,128)(2,1)} %bitcast.11, f32[4,128]{1,0:T(4,128)} %bitcast.15, bf16[512,128]{1,0:T(8,128)(2,1)} %bitcast.12, ...), custom_call_target="tpu_custom_call" | custom-call | tf_op jit(solution)/shard_map/pallas_call | solution.py:253
  15.8 0.7 %shard_map.95 = (bf16[512,128]{1,0:T(8,128)(2,1)}, bf16[128,128]{1,0:T(8,128)(2,1)}, bf16[128,128]{1,0:T(8,128)(2,1)}) custom-call(bf16[512,128]{1,0:T(8,128)(2,1)S(1)} %get-tuple-element.8.dq_ref, bf16[2,128,128]{2,1,0:T(8,128)(2,1)S(1)} %get-tuple-element.9.kv_ref), custom_call_target="tpu_custom_call" | custom-call | tf_op jit(solution)/shard_map/pallas_call | solution.py:294
where the time goes:
time: 16.7 us; the launch traced here: 16.5 us
  Pallas kernels  15.8 us (95%)
  between operations  0.64 us (4%)
    pallas_call x1, Pallas kernels, body(): pl.pallas_call(functools.partial(kernel, n, heads), out_shape=(pltpu.VMEM...  15.1 us
    pallas_call x1, Pallas kernels, body(): pl.pallas_call(store_kernel, out_shape=(jax.ShapeDtypeStruct((rows, width...  0.7 us

commit v1 on v0

v1 whole, which is shorter than its diff:
```python
import functools
import math

import jax
import jax.numpy as jnp
from jax import lax
from jax.experimental import pallas as pl
from jax.experimental.pallas import tpu as pltpu
from jax.sharding import PartitionSpec as P

MESH = pl.DeviceIdType.MESH
F32 = jnp.float32
BF16 = jnp.bfloat16
NT = (((1,), (1,)), ((), ()))
TN = (((0,), (0,)), ((), ()))
LOG2E = math.log2(math.e)


def dot(a, b, dims=(((1,), (0,)), ((), ()))):
    return lax.dot_general(a, b, dims, preferred_element_type=F32)


def kernel(
    n,
    heads,
    q_hbm,
    k_hbm,
    v_hbm,
    o_hbm,
    l_hbm,
    g_hbm,
    order_hbm,
    dq_ref,
    kv_ref,
    qs,
    gs,
    os_,
    ls,
    mine,
    kv,
    stat,
    ds_all,
    send_buf,
    recv_buf,
    dq_send,
    dq_recv,
    order,
    load_sem,
    pair_send,
    pair_recv,
    kv_send,
    kv_recv,
    grad_send,
    grad_recv,
    fin_send,
    fin_recv,
):
    me = lax.axis_index("inner")
    core = lax.axis_index("head")
    m = n // 2
    half, width = kv.shape[3], kv.shape[4]
    rows = qs.shape[1]
    scale = 1.0 / math.sqrt(width)
    partner = {"head": 1 - core}
    top, low = me // m, me % m

    def flip(value, bits):
        for k in range(m.bit_length()):
            if bits >> k & 1:
                value = value + (1 - 2 * ((value // 2**k) % 2)) * 2**k
        return value

    def flip_low(value, on):
        return value + on * (1 - 2 * (value % 2))

    inner_first = (low % 2 + top) % 2 * core if m > 1 else 0
    far_top = top + core - 2 * top * core
    slots = [flip_low(j, inner_first) if m > 1 else j for j in range(m)]
    peers = [
        far_top * m + (flip_low(flip(low, j), inner_first) if m > 1 else low)
        for j in range(m)
    ]

    barrier = pltpu.get_barrier_semaphore()

    def greet(inner, head):
        pl.semaphore_signal(
            barrier, inc=1, device_id={"inner": inner, "head": head}, device_id_type=MESH
        )

    @pl.when(core == 1)
    def _():
        for j in reversed(range(m)):
            greet(peers[j], 1)
        for j in range(m):
            greet(top * m + flip(low, j), 0)

    @pl.when(core == 0)
    def _():
        greet(me, 1)
        for j in range(1, m):
            greet(peers[j], 0)

    loads = [
        pltpu.make_async_copy(src, dst, load_sem.at[i])
        for i, (src, dst) in enumerate(
            (
                (k_hbm.at[0:half], mine.at[0, 0]),
                (v_hbm.at[0:half], mine.at[0, 1]),
                (k_hbm.at[half:], mine.at[1, 0]),
                (v_hbm.at[half:], mine.at[1, 1]),
                (q_hbm, qs.at[0]),
                (g_hbm, gs.at[0]),
                (o_hbm, os_),
                (l_hbm, ls),
                (order_hbm, order),
            )
        )
    ]
    for load in loads:
        load.start()

    @pl.when(core == 0)
    def _():
        for h in range(2):
            span = pl.ds(h * half, half)
            pltpu.make_async_copy(k_hbm.at[span], kv.at[0, h, 0], kv_recv.at[0, h]).start()
            pltpu.make_async_copy(v_hbm.at[span], kv.at[0, h, 1], kv_recv.at[0, h]).start()

    def kv_copy(j, h):
        return pltpu.make_async_remote_copy(
            src_ref=mine.at[h],
            dst_ref=kv.at[slots[j], h],
            send_sem=kv_send.at[j, h],
            recv_sem=kv_recv.at[slots[j], h],
            device_id={"inner": peers[j]},
            device_id_type=MESH,
        )

    for load in loads[:4]:
        load.wait()
    pl.semaphore_wait(barrier, jnp.where(core == 1, m + 1, n - 1))
    for j in reversed(range(1, m)):
        for h in range(2):
            kv_copy(j, h).start()

    @pl.when(core == 1)
    def _():
        for h in range(2):
            kv_copy(0, h).start()

    def pair_copy(i, src, dst):
        return pltpu.make_async_remote_copy(
            src_ref=src,
            dst_ref=dst,
            send_sem=pair_send.at[i],
            recv_sem=pair_recv.at[i],
            device_id=partner,
            device_id_type=MESH,
        )

    pair_copies = []
    for i, ref in enumerate((qs, gs)):
        loads[4 + i].wait()
        copy = pair_copy(i, ref.at[0], ref.at[1])
        copy.start()
        pair_copies.append(copy)
    loads[6].wait()
    loads[7].wait()

    toks = rows // heads
    col = lax.broadcasted_iota(jnp.int32, (toks, rows), 1)
    spread = jnp.where(
        col // heads == lax.broadcasted_iota(jnp.int32, (toks, rows), 0), 1.0, 0.0
    )
    head_of = lax.broadcasted_iota(jnp.int32, (heads, rows), 1) % heads
    pick = head_of == lax.broadcasted_iota(jnp.int32, (heads, rows), 0)
    ones = jnp.ones((8, width), BF16)
    total = jnp.dot(
        ls[...], spread, preferred_element_type=F32, precision=lax.Precision.HIGHEST
    )
    total = jnp.sum(jnp.where(pick, total, 0.0), axis=0, keepdims=True)
    prod = os_[...].astype(F32) * gs[0].astype(F32)
    high = prod.astype(BF16)
    rest = (prod - high.astype(F32)).astype(BF16)
    delta = dot(ones, high, NT) + dot(ones, rest, NT)
    stat[0, 0:1] = total * LOG2E
    stat[0, 1:2] = delta[0:1]
    copy = pair_copy(2, stat.at[0], stat.at[1])
    copy.start()
    pair_copies.append(copy)

    loads[8].wait()
    tok = (lax.broadcasted_iota(jnp.int32, (1, rows), 1)) // heads
    q_span = jnp.where(tok < half, order[2 * me], order[2 * me + 1])
    q_pos = q_span * half + tok % half
    q_span = jnp.concatenate([q_span, q_span], axis=1)
    q_pos = jnp.concatenate([q_pos, q_pos], axis=1)
    key_row = lax.broadcasted_iota(jnp.int32, (half, 1), 0)

    for copy in pair_copies:
        copy.wait_recv()
    totals = jnp.concatenate([stat[0, 0:1], stat[1, 0:1]], axis=1)
    deltas = jnp.concatenate([stat[0, 1:2], stat[1, 1:2]], axis=1)

    def block(j, h):
        k_span = order[2 * peers[j] + h]
        queries = qs[...].reshape(2 * rows, width)
        grads = gs[...].reshape(2 * rows, width)
        scores = dot(kv[slots[j], h, 0], queries, NT)
        grad_probs = dot(kv[slots[j], h, 1], grads, NT)
        if j == 0:
            visible = k_span * half + key_row <= q_pos
            probs = jnp.exp2(
                jnp.where(visible, scores * (scale * LOG2E) - totals, -jnp.inf)
            )
        else:
            shift = jnp.where(k_span < q_span, totals, jnp.inf)
            probs = jnp.exp2(scores * (scale * LOG2E) - shift)
        grad_scores = (probs * (grad_probs - deltas) * scale).astype(BF16)
        ds_all[j, h] = grad_scores
        yield 1, dot(probs.astype(BF16), grads)
        yield 0, dot(grad_scores, queries)

    def grad_copy(j, h, i):
        at = core * m + slots[j]
        return pltpu.make_async_remote_copy(
            src_ref=send_buf.at[j, h, i],
            dst_ref=recv_buf.at[at, h, i],
            send_sem=grad_send.at[j, h, i],
            recv_sem=grad_recv.at[at, h, i],
            device_id={"inner": peers[j], "head": 1},
            device_id_type=MESH,
        )

    for j in range(m):
        for h in range(2):
            kv_copy(j, h).wait_recv()
            for i, grad in block(j, h):
                send_buf[j, h, i] = grad.astype(BF16)
                grad_copy(j, h, i).start()

    def query_grad(i):
        total = None
        for j in range(m):
            for h in range(2):
                term = dot(
                    ds_all[j, h, :, i * rows : (i + 1) * rows], kv[slots[j], h, 0], TN
                )
                total = term if total is None else total + term
        return total

    dq_send[...] = query_grad(1)
    dq_copy = pair_copy(3, dq_send, dq_recv)
    dq_copy.start()
    own_grad = query_grad(0)
    dq_copy.wait_recv()
    dq_ref[...] = (own_grad + dq_recv[...]).astype(BF16)

    def fin_copy(h, i):
        span = kv_ref.at[i, pl.ds(h * half, half)]
        return pltpu.make_async_remote_copy(
            src_ref=span,
            dst_ref=span,
            send_sem=fin_send.at[h, i],
            recv_sem=fin_recv.at[h, i],
            device_id=partner,
            device_id_type=MESH,
        )

    @pl.when(core == 1)
    def _():
        for h in range(2):
            for i in (1, 0):
                total = None
                for d in range(n):
                    pltpu.make_async_remote_copy(
                        src_ref=send_buf.at[0, h, i],
                        dst_ref=recv_buf.at[d, h, i],
                        send_sem=grad_send.at[0, h, i],
                        recv_sem=grad_recv.at[d, h, i],
                        device_id=partner,
                        device_id_type=MESH,
                    ).wait_recv()
                    term = recv_buf[d, h, i].astype(F32)
                    total = term if total is None else total + term
                kv_ref[i, h * half : (h + 1) * half] = total.astype(BF16)
                fin_copy(h, i).start()
        for h in range(2):
            kv_copy(0, h).wait_send()
            for i in (1, 0):
                fin_copy(h, i).wait_send()

    for j in range(m):
        for h in range(2):
            if j:
                kv_copy(j, h).wait_send()
            for i in (1, 0):
                grad_copy(j, h, i).wait_send()
    for copy in pair_copies + [dq_copy]:
        copy.wait_send()

    @pl.when(core == 0)
    def _():
        for h in range(2):
            for i in (1, 0):
                fin_copy(h, i).wait_recv()


def store_kernel(dq_ref, kv_ref, dq_hbm, dk_hbm, dv_hbm, sem):
    pairs = ((dq_ref, dq_hbm), (kv_ref.at[0], dk_hbm), (kv_ref.at[1], dv_hbm))
    copies = [pltpu.make_async_copy(a, b, sem.at[i]) for i, (a, b) in enumerate(pairs)]
    for copy in copies:
        copy.start()
    for copy in copies:
        copy.wait()


def body(n, queries, keys, values, out, log_total, d_out, span_order):
    _, toks, heads, width = queries.shape
    rows = toks * heads
    half = toks // 2
    m = n // 2
    flat = lambda x: x.reshape(rows, width)
    anywhere = pl.BlockSpec(memory_space=pltpu.HBM)
    in_vmem = pl.BlockSpec(memory_space=pltpu.VMEM)
    dq, dkv = pl.pallas_call(
        functools.partial(kernel, n, heads),
        out_shape=(
            pltpu.VMEM((rows, width), BF16),
            pltpu.VMEM((2, toks, width), BF16),
        ),
        in_specs=[anywhere] * 7,
        out_specs=(in_vmem,) * 2,
        scratch_shapes=[
            pltpu.VMEM((2, rows, width), BF16),
            pltpu.VMEM((2, rows, width), BF16),
            pltpu.VMEM((rows, width), BF16),
            pltpu.VMEM((heads, toks), F32),
            pltpu.VMEM((2, 2, half, width), BF16),
            pltpu.VMEM((m, 2, 2, half, width), BF16),
            pltpu.VMEM((2, 8, rows), F32),
            pltpu.VMEM((m, 2, half, 2 * rows), BF16),
            pltpu.VMEM((m, 2, 2, half, width), BF16),
            pltpu.VMEM((n, 2, 2, half, width), BF16),
            pltpu.VMEM((rows, width), F32),
            pltpu.VMEM((rows, width), F32),
            pltpu.SMEM((span_order.shape[1],), jnp.int32),
            pltpu.SemaphoreType.DMA((9,)),
            pltpu.SemaphoreType.DMA((4,)),
            pltpu.SemaphoreType.DMA((4,)),
            pltpu.SemaphoreType.DMA((m, 2)),
            pltpu.SemaphoreType.DMA((m, 2)),
            pltpu.SemaphoreType.DMA((m, 2, 2)),
            pltpu.SemaphoreType.DMA((n, 2, 2)),
            pltpu.SemaphoreType.DMA((2, 2)),
            pltpu.SemaphoreType.DMA((2, 2)),
        ],
        compiler_params=pltpu.CompilerParams(collective_id=0, has_side_effects=True),
    )(
        flat(queries),
        keys[0],
        values[0],
        flat(out),
        log_total[0],
        flat(d_out),
        span_order[0],
    )
    dq, dk, dv = pl.pallas_call(
        store_kernel,
        out_shape=(
            jax.ShapeDtypeStruct((rows, width), BF16),
            jax.ShapeDtypeStruct((toks, width), BF16),
            jax.ShapeDtypeStruct((toks, width), BF16),
        ),
        in_specs=[in_vmem] * 2,
        out_specs=(anywhere,) * 3,
        scratch_shapes=[pltpu.SemaphoreType.DMA((3,))],
        compiler_params=pltpu.CompilerParams(vmem_limit_bytes=2**20),
    )(dq, dkv)
    return dq.reshape(queries.shape), dk[None], dv[None]


def solution(mesh):
    seq = ("groups", "outer")
    wide = P(seq, "inner", "head", None)
    narrow = P(seq, "inner", None)
    return jax.shard_map(
        functools.partial(body, mesh.shape["inner"]),
        mesh=mesh,
        in_specs=(wide, narrow, narrow, wide, P(seq, "head", "inner"), wide, P(seq, None)),
        out_specs=(wide, narrow, narrow),
        check_vma=False,
    )
```

time: 16.7 us -> 16.4 us (0.982)
  Pallas kernels: 15.8 us -> 15.5 us
    pallas_call x1, Pallas kernels: 15.1 us -> 14.8 us  [body(): pl.pallas_call(functools.partial(kernel, n, heads), out_shape=(pltpu.VMEM...]
where the time goes in v1:
time: 16.4 us; the launch traced here: 16.1 us
  Pallas kernels  15.5 us (95%)
  between operations  0.64 us (4%)
    pallas_call x1, Pallas kernels, body(): pl.pallas_call(functools.partial(kernel, n, heads), out_shape=(pltpu.VMEM...  14.8 us
    pallas_call x1, Pallas kernels, body(): pl.pallas_call(store_kernel, out_shape=(jax.ShapeDtypeStruct((rows, width...  0.7 us

profile of v1, /device:TPU:0, one launch (start us, length us, event | category | flops | bytes accessed | tf_op | source)
XLA Modules:
  0.0 16.1 jit_solution(10120075898951873590)
XLA Ops:
  0.6 14.8 %shard_map.94 = (bf16[512,128]{1,0:T(8,128)(2,1)S(1)}, bf16[2,128,128]{2,1,0:T(8,128)(2,1)S(1)}) custom-call(bf16[512,128]{1,0:T(8,128)(2,1)} %bitcast.10, bf16[128,128]{1,0:T(8,128)(2,1)} %bitcast.13, bf16[128,128]{1,0:T(8,128)(2,1)} %bitcast.14, bf16[512,128]{1,0:T(8,128)(2,1)} %bitcast.11, f32[4,128]{1,0:T(4,128)} %bitcast.15, bf16[512,128]{1,0:T(8,128)(2,1)} %bitcast.12, ...), custom_call_target="tpu_custom_call" | custom-call | tf_op jit(solution)/shard_map/pallas_call | solution.py:327
  15.4 0.7 %shard_map.95 = (bf16[512,128]{1,0:T(8,128)(2,1)}, bf16[128,128]{1,0:T(8,128)(2,1)}, bf16[128,128]{1,0:T(8,128)(2,1)}) custom-call(bf16[512,128]{1,0:T(8,128)(2,1)S(1)} %get-tuple-element.8.dq_ref, bf16[2,128,128]{2,1,0:T(8,128)(2,1)S(1)} %get-tuple-element.9.kv_ref), custom_call_target="tpu_custom_call" | custom-call | tf_op jit(solution)/shard_map/pallas_call | solution.py:369

commit v2 on v1

v2 whole, which is shorter than its diff:
```python
import functools
import math

import jax
import jax.numpy as jnp
from jax import lax
from jax.experimental import pallas as pl
from jax.experimental.pallas import tpu as pltpu
from jax.sharding import PartitionSpec as P

MESH = pl.DeviceIdType.MESH
F32 = jnp.float32
BF16 = jnp.bfloat16
NT = (((1,), (1,)), ((), ()))
TN = (((0,), (0,)), ((), ()))
LOG2E = math.log2(math.e)


def dot(a, b, dims=(((1,), (0,)), ((), ()))):
    return lax.dot_general(a, b, dims, preferred_element_type=F32)


def kernel(
    n,
    heads,
    q_hbm,
    k_hbm,
    v_hbm,
    o_hbm,
    l_hbm,
    g_hbm,
    order_hbm,
    dq_ref,
    kv_ref,
    qg,
    os_,
    ls,
    mine,
    kv,
    stat,
    ds_all,
    send_buf,
    recv_buf,
    dq_send,
    dq_recv,
    order,
    sem,
    pair_recv,
    kv_recv,
    grad_recv,
):
    me = lax.axis_index("inner")
    core = lax.axis_index("head")
    m = n // 2
    split = m + m // 2
    half, width = kv.shape[3], kv.shape[4]
    rows = qg.shape[2]
    scale = 1.0 / math.sqrt(width)
    partner = {"head": 1 - core}

    def chip(d):
        at = me
        for k in range(n.bit_length()):
            if d >> k & 1:
                at = at + (1 - 2 * ((me // 2**k) % 2)) * 2**k
        return at

    owners = [chip(j) + core * (chip(n - 1 - j) - chip(j)) for j in range(m)]

    barrier = pltpu.get_barrier_semaphore()

    def greet(inner, head):
        pl.semaphore_signal(
            barrier, inc=1, device_id={"inner": inner, "head": head}, device_id_type=MESH
        )

    @pl.when(core == 1)
    def _():
        for d in reversed(range(split, n)):
            greet(chip(d), 1)
        for d in reversed(range(m, split)):
            greet(chip(d), 0)
        greet(me, 0)

    @pl.when(core == 0)
    def _():
        for d in range(1, m):
            greet(chip(d), 0)
        greet(me, 1)

    loads = [
        pltpu.make_async_copy(src, dst, sem.at[i])
        for src, dst, i in (
            (k_hbm.at[0:half], mine.at[0, 0], 0),
            (v_hbm.at[0:half], mine.at[0, 1], 0),
            (k_hbm.at[half:], mine.at[1, 0], 0),
            (v_hbm.at[half:], mine.at[1, 1], 0),
            (q_hbm, qg.at[0, 0], 1),
            (g_hbm, qg.at[0, 1], 1),
            (o_hbm, os_, 2),
            (l_hbm, ls, 3),
            (order_hbm, order, 4),
        )
    ]
    for load in loads:
        load.start()

    @pl.when(core == 0)
    def _():
        for h in range(2):
            span = pl.ds(h * half, half)
            pltpu.make_async_copy(k_hbm.at[span], kv.at[0, h, 0], kv_recv.at[0, h]).start()
            pltpu.make_async_copy(v_hbm.at[span], kv.at[0, h, 1], kv_recv.at[0, h]).start()

    def remote(src, dst, send, recv, inner, head):
        return pltpu.make_async_remote_copy(
            src_ref=src,
            dst_ref=dst,
            send_sem=sem.at[send],
            recv_sem=recv,
            device_id={"inner": inner, "head": head},
            device_id_type=MESH,
        )

    def wait_bytes(ref, recv):
        remote(ref, ref, 0, recv, me, 1 - core).wait_recv()

    def wait_sent(ref, send):
        remote(ref, ref, send, pair_recv.at[0], me, 1 - core).wait_send()

    def kv_send(d):
        for h in range(2):
            slot = d if d < m else n - 1 - d
            remote(
                mine.at[h], kv.at[slot, h], 0, kv_recv.at[slot, h], chip(d), int(d >= m)
            ).start()

    wait_bytes(mine, sem.at[0])
    pl.semaphore_wait(barrier, jnp.where(core == 1, n - split + 1, split))

    @pl.when(core == 1)
    def _():
        for d in reversed(range(split, n)):
            kv_send(d)

    @pl.when(core == 0)
    def _():
        for d in reversed(range(1, split)):
            kv_send(d)

    wait_bytes(qg.at[0], sem.at[1])
    remote(qg.at[0], qg.at[1], 1, pair_recv.at[0], me, 1 - core).start()
    loads[6].wait()
    loads[7].wait()

    toks = rows // heads
    col = lax.broadcasted_iota(jnp.int32, (toks, rows), 1)
    spread = jnp.where(
        col // heads == lax.broadcasted_iota(jnp.int32, (toks, rows), 0), 1.0, 0.0
    )
    head_of = lax.broadcasted_iota(jnp.int32, (heads, rows), 1) % heads
    pick = head_of == lax.broadcasted_iota(jnp.int32, (heads, rows), 0)
    ones = jnp.ones((8, width), BF16)
    total = jnp.dot(
        ls[...], spread, preferred_element_type=F32, precision=lax.Precision.HIGHEST
    )
    total = jnp.sum(jnp.where(pick, total, 0.0), axis=0, keepdims=True)
    prod = os_[...].astype(F32) * qg[0, 1].astype(F32)
    high = prod.astype(BF16)
    rest = (prod - high.astype(F32)).astype(BF16)
    delta = dot(ones, high, NT) + dot(ones, rest, NT)
    stat[0, 0:1] = total * LOG2E
    stat[0, 1:2] = delta[0:1]
    remote(stat.at[0], stat.at[1], 2, pair_recv.at[1], me, 1 - core).start()

    loads[8].wait()
    tok = (lax.broadcasted_iota(jnp.int32, (1, rows), 1)) // heads
    q_span = jnp.where(tok < half, order[2 * me], order[2 * me + 1])
    q_pos = q_span * half + tok % half
    q_span = jnp.concatenate([q_span, q_span], axis=1)
    q_pos = jnp.concatenate([q_pos, q_pos], axis=1)
    key_row = lax.broadcasted_iota(jnp.int32, (half, 1), 0)

    with jax.named_scope("w_pair"):
        wait_bytes(qg.at[1], pair_recv.at[0])
        wait_bytes(stat.at[1], pair_recv.at[1])
    totals = jnp.concatenate([stat[0, 0:1], stat[1, 0:1]], axis=1)
    deltas = jnp.concatenate([stat[0, 1:2], stat[1, 1:2]], axis=1)

    def block(j, h):
        k_span = order[2 * owners[j] + h]
        queries = qg[:, 0].reshape(2 * rows, width)
        grads = qg[:, 1].reshape(2 * rows, width)
        scores = dot(kv[j, h, 0], queries, NT)
        grad_probs = dot(kv[j, h, 1], grads, NT)
        if j == 0:
            visible = k_span * half + key_row <= q_pos
            probs = jnp.exp2(
                jnp.where(visible, scores * (scale * LOG2E) - totals, -jnp.inf)
            )
        else:
            shift = jnp.where(k_span < q_span, totals, jnp.inf)
            probs = jnp.exp2(scores * (scale * LOG2E) - shift)
        grad_scores = (probs * (grad_probs - deltas) * scale).astype(BF16)
        ds_all[j, h] = grad_scores
        yield 1, dot(probs.astype(BF16), grads)
        yield 0, dot(grad_scores, queries)

    for j in range(m):
        for h in range(2):
            with jax.named_scope(f"w_kv{j}{h}"):
                wait_bytes(kv.at[j, h], kv_recv.at[j, h])
            with jax.named_scope(f"block{j}{h}"):
                for i, grad in block(j, h):
                    send_buf[j, h, i] = grad.astype(BF16)
                    at = j + core * (n - 1 - 2 * j)
                    remote(
                        send_buf.at[j, h, i],
                        recv_buf.at[at, h, i],
                        3,
                        grad_recv.at[at, h],
                        owners[j],
                        1,
                    ).start()

    def query_grad(i):
        total = None
        for j in range(m):
            for h in range(2):
                term = dot(
                    ds_all[j, h, :, i * rows : (i + 1) * rows], kv[j, h, 0], TN
                )
                total = term if total is None else total + term
        return total

    with jax.named_scope("dq"):
        dq_send[...] = query_grad(1)
        dq_copy = remote(dq_send, dq_recv, 4, pair_recv.at[2], me, 1 - core)
        dq_copy.start()
        own_grad = query_grad(0)
    with jax.named_scope("w_dq"):
        dq_copy.wait_recv()
    dq_ref[...] = (own_grad + dq_recv[...]).astype(BF16)

    with jax.named_scope("w_sends"):
        wait_sent(qg.at[0], 1)
        wait_sent(stat.at[0], 2)
        wait_sent(send_buf, 3)
        dq_copy.wait_send()

        @pl.when(core == 1)
        def _():
            wait_sent(recv_buf.at[0 : n - split], 0)

        @pl.when(core == 0)
        def _():
            if split > 1:
                wait_sent(recv_buf.at[1:split], 0)

    @pl.when(core == 1)
    def _():
        for h in range(2):
            total = [None, None]
            for d in range(n):
                with jax.named_scope(f"w_g{d}_{h}"):
                    wait_bytes(recv_buf.at[d, h], grad_recv.at[d, h])
                for i in range(2):
                    term = recv_buf[d, h, i].astype(F32)
                    total[i] = term if d == 0 else total[i] + term
            for i in range(2):
                span = kv_ref.at[i, pl.ds(h * half, half)]
                span[...] = total[i].astype(BF16)
                remote(span, span, 5, pair_recv.at[3], me, 0).start()
        with jax.named_scope("w_finsend"):
            wait_sent(kv_ref, 5)

    @pl.when(core == 0)
    def _():
        with jax.named_scope("w_fin"):
            wait_bytes(kv_ref, pair_recv.at[3])


def store_kernel(dq_ref, kv_ref, dq_hbm, dk_hbm, dv_hbm, sem):
    pairs = ((dq_ref, dq_hbm), (kv_ref.at[0], dk_hbm), (kv_ref.at[1], dv_hbm))
    copies = [pltpu.make_async_copy(a, b, sem.at[i]) for i, (a, b) in enumerate(pairs)]
    for copy in copies:
        copy.start()
    for copy in copies:
        copy.wait()


def body(n, queries, keys, values, out, log_total, d_out, span_order):
    _, toks, heads, width = queries.shape
    rows = toks * heads
    half = toks // 2
    m = n // 2
    flat = lambda x: x.reshape(rows, width)
    anywhere = pl.BlockSpec(memory_space=pltpu.HBM)
    in_vmem = pl.BlockSpec(memory_space=pltpu.VMEM)
    dq, dkv = pl.pallas_call(
        functools.partial(kernel, n, heads),
        out_shape=(
            pltpu.VMEM((rows, width), BF16),
            pltpu.VMEM((2, toks, width), BF16),
        ),
        in_specs=[anywhere] * 7,
        out_specs=(in_vmem,) * 2,
        scratch_shapes=[
            pltpu.VMEM((2, 2, rows, width), BF16),
            pltpu.VMEM((rows, width), BF16),
            pltpu.VMEM((heads, toks), F32),
            pltpu.VMEM((2, 2, half, width), BF16),
            pltpu.VMEM((m, 2, 2, half, width), BF16),
            pltpu.VMEM((2, 8, rows), F32),
            pltpu.VMEM((m, 2, half, 2 * rows), BF16),
            pltpu.VMEM((m, 2, 2, half, width), BF16),
            pltpu.VMEM((n, 2, 2, half, width), BF16),
            pltpu.VMEM((rows, width), F32),
            pltpu.VMEM((rows, width), F32),
            pltpu.SMEM((span_order.shape[1],), jnp.int32),
            pltpu.SemaphoreType.DMA((6,)),
            pltpu.SemaphoreType.DMA((4,)),
            pltpu.SemaphoreType.DMA((m, 2)),
            pltpu.SemaphoreType.DMA((n, 2)),
        ],
        compiler_params=pltpu.CompilerParams(collective_id=0, has_side_effects=True),
    )(
        flat(queries),
        keys[0],
        values[0],
        flat(out),
        log_total[0],
        flat(d_out),
        span_order[0],
    )
    dq, dk, dv = pl.pallas_call(
        store_kernel,
        out_shape=(
            jax.ShapeDtypeStruct((rows, width), BF16),
            jax.ShapeDtypeStruct((toks, width), BF16),
            jax.ShapeDtypeStruct((toks, width), BF16),
        ),
        in_specs=[in_vmem] * 2,
        out_specs=(anywhere,) * 3,
        scratch_shapes=[pltpu.SemaphoreType.DMA((3,))],
        compiler_params=pltpu.CompilerParams(vmem_limit_bytes=2**20),
    )(dq, dkv)
    return dq.reshape(queries.shape), dk[None], dv[None]


def solution(mesh):
    seq = ("groups", "outer")
    wide = P(seq, "inner", "head", None)
    narrow = P(seq, "inner", None)
    return jax.shard_map(
        functools.partial(body, mesh.shape["inner"]),
        mesh=mesh,
        in_specs=(wide, narrow, narrow, wide, P(seq, "head", "inner"), wide, P(seq, None)),
        out_specs=(wide, narrow, narrow),
        check_vma=False,
    )
```

time: 16.4 us -> 14.6 us (0.89)
  Pallas kernels: 15.5 us -> 13.8 us
    pallas_call x1, Pallas kernels: 14.8 us -> 13.1 us  [body(): pl.pallas_call(functools.partial(kernel, n, heads), out_shape=(pltpu.VMEM...]
where the time goes in v2:
time: 14.6 us; the launch traced here: 14.4 us
  Pallas kernels  13.8 us (95%)
  between operations  0.64 us (4%)
    pallas_call x1, Pallas kernels, body(): pl.pallas_call(functools.partial(kernel, n, heads), out_shape=(pltpu.VMEM...  13.1 us
    pallas_call x1, Pallas kernels, body(): pl.pallas_call(store_kernel, out_shape=(jax.ShapeDtypeStruct((rows, width...  0.7 us

profile of v2, /device:TPU:0, one launch (start us, length us, event | category | flops | bytes accessed | tf_op | source)
XLA Modules:
  0.0 14.4 jit_solution(13244548727438457965)
XLA Ops:
  0.6 13.1 %shard_map.94 = (bf16[512,128]{1,0:T(8,128)(2,1)S(1)}, bf16[2,128,128]{2,1,0:T(8,128)(2,1)S(1)}) custom-call(bf16[512,128]{1,0:T(8,128)(2,1)} %bitcast.10, bf16[128,128]{1,0:T(8,128)(2,1)} %bitcast.13, bf16[128,128]{1,0:T(8,128)(2,1)} %bitcast.14, bf16[512,128]{1,0:T(8,128)(2,1)} %bitcast.11, f32[4,128]{1,0:T(4,128)} %bitcast.15, bf16[512,128]{1,0:T(8,128)(2,1)} %bitcast.12, ...), custom_call_target="tpu_custom_call" | custom-call | tf_op jit(solution)/shard_map/pallas_call | solution.py:300
  13.7 0.7 %shard_map.95 = (bf16[512,128]{1,0:T(8,128)(2,1)}, bf16[128,128]{1,0:T(8,128)(2,1)}, bf16[128,128]{1,0:T(8,128)(2,1)}) custom-call(bf16[512,128]{1,0:T(8,128)(2,1)S(1)} %get-tuple-element.8.dq_ref, bf16[2,128,128]{2,1,0:T(8,128)(2,1)S(1)} %get-tuple-element.9.kv_ref), custom_call_target="tpu_custom_call" | custom-call | tf_op jit(solution)/shard_map/pallas_call | solution.py:336

commit v3 on v2

v3 whole, which is shorter than its diff:
```python
import functools
import math

import jax
import jax.numpy as jnp
from jax import lax
from jax.experimental import pallas as pl
from jax.experimental.pallas import tpu as pltpu
from jax.sharding import PartitionSpec as P

MESH = pl.DeviceIdType.MESH
F32 = jnp.float32
BF16 = jnp.bfloat16
NT = (((1,), (1,)), ((), ()))
TN = (((0,), (0,)), ((), ()))
LOG2E = math.log2(math.e)


def dot(a, b, dims=(((1,), (0,)), ((), ()))):
    return lax.dot_general(a, b, dims, preferred_element_type=F32)


def kernel(
    n,
    heads,
    q_hbm,
    k_hbm,
    v_hbm,
    o_hbm,
    l_hbm,
    g_hbm,
    order_hbm,
    dq_ref,
    kv_ref,
    qg,
    os_,
    ls,
    mine,
    kv,
    stat,
    ds_all,
    send_buf,
    recv_buf,
    part,
    dq_send,
    dq_recv,
    order,
    sem,
    pair_recv,
    kv_recv,
    grad_recv,
    entered,
):
    me = lax.axis_index("inner")
    core = lax.axis_index("head")
    m = n // 2
    split = m + m // 2
    toks, width = kv.shape[2], kv.shape[3]
    half = toks // 2
    rows = qg.shape[2]
    scale = 1.0 / math.sqrt(width)
    partner = {"head": 1 - core}

    def chip(d):
        at = me
        for k in range(n.bit_length()):
            if d >> k & 1:
                at = at + (1 - 2 * ((me // 2**k) % 2)) * 2**k
        return at

    owners = [chip(j) + core * (chip(n - 1 - j) - chip(j)) for j in range(m)]

    barrier = pltpu.get_barrier_semaphore()

    def greet(inner, head, when=None):
        def signal():
            pl.semaphore_signal(
                barrier, inc=1, device_id={"inner": inner, "head": head}, device_id_type=MESH
            )

        signal() if when is None else pl.when(when)(signal)

    @pl.when(core == 1)
    def _():
        greet(0, 1, me == 1)
        for d in reversed(range(split, n)):
            greet(chip(d), 1, chip(d) != 0)
        for d in reversed(range(m, split)):
            greet(chip(d), 0)
        greet(me, 0)

    @pl.when(core == 0)
    def _():
        for d in range(1, m):
            greet(chip(d), 0, chip(d) != 0)
        greet(me, 1)

    loads = [
        pltpu.make_async_copy(src, dst, sem.at[i])
        for src, dst, i in (
            (k_hbm, mine.at[0], 0),
            (v_hbm, mine.at[1], 0),
            (q_hbm, qg.at[0, 0], 1),
            (g_hbm, qg.at[0, 1], 1),
            (o_hbm, os_, 2),
            (l_hbm, ls, 3),
            (order_hbm, order, 4),
        )
    ]
    for load in loads:
        load.start()

    @pl.when(core == 0)
    def _():
        pltpu.make_async_copy(k_hbm, kv.at[0, 0], kv_recv.at[0, 0]).start()
        pltpu.make_async_copy(v_hbm, kv.at[0, 1], kv_recv.at[0, 1]).start()

    def remote(src, dst, send, recv, inner, head):
        return pltpu.make_async_remote_copy(
            src_ref=src,
            dst_ref=dst,
            send_sem=sem.at[send],
            recv_sem=recv,
            device_id={"inner": inner, "head": head},
            device_id_type=MESH,
        )

    def wait_bytes(ref, recv):
        remote(ref, ref, 0, recv, me, 1 - core).wait_recv()

    def wait_sent(ref, send):
        remote(ref, ref, send, pair_recv.at[0], me, 1 - core).wait_send()

    def slot_of(d):
        return d if d < m else n - 1 - d

    def kv_send(d):
        for i in range(2):
            place = (slot_of(d), i)
            remote(
                mine.at[i], kv.at[place], 0, kv_recv.at[place], chip(d), int(d >= m)
            ).start()

    wait_bytes(mine, sem.at[0])
    sent = jnp.where(
        me == 0,
        jnp.where(core == 1, 1, split - m),
        jnp.where(core == 1, n - split, split - 1),
    )
    pl.semaphore_wait(barrier, 1 + sent)

    @pl.when(me == 0)
    def _():
        @pl.when(core == 1)
        def _():
            for i in range(2):
                remote(mine.at[i], kv.at[m, i], 0, kv_recv.at[m, i], 1, 1).start()

    @pl.when(me != 0)
    def _():
        @pl.when(core == 1)
        def _():
            for d in reversed(range(split, n)):
                kv_send(d)

        @pl.when(core == 0)
        def _():
            @pl.when(me == 1)
            def _():
                pl.semaphore_signal(
                    entered, inc=1, device_id={"inner": me, "head": 1}, device_id_type=MESH
                )

            for d in range(1, m):
                kv_send(d)

    def middle_sends(when):
        @pl.when(jnp.logical_and(core == 0, when))
        def _():
            for d in range(m, split):
                kv_send(d)

    middle_sends(me != 1)

    wait_bytes(qg.at[0], sem.at[1])
    remote(qg.at[0], qg.at[1], 1, pair_recv.at[0], me, 1 - core).start()
    loads[4].wait()
    loads[5].wait()

    col = lax.broadcasted_iota(jnp.int32, (toks, rows), 1)
    spread = jnp.where(
        col // heads == lax.broadcasted_iota(jnp.int32, (toks, rows), 0), 1.0, 0.0
    )
    head_of = lax.broadcasted_iota(jnp.int32, (heads, rows), 1) % heads
    pick = head_of == lax.broadcasted_iota(jnp.int32, (heads, rows), 0)
    ones = jnp.ones((8, width), BF16)
    total = jnp.dot(
        ls[...], spread, preferred_element_type=F32, precision=lax.Precision.HIGHEST
    )
    total = jnp.sum(jnp.where(pick, total, 0.0), axis=0, keepdims=True)
    prod = os_[...].astype(F32) * qg[0, 1].astype(F32)
    high = prod.astype(BF16)
    rest = (prod - high.astype(F32)).astype(BF16)
    delta = dot(ones, high, NT) + dot(ones, rest, NT)
    stat[0, 0:1] = total * LOG2E
    stat[0, 1:2] = delta[0:1]
    remote(stat.at[0], stat.at[1], 2, pair_recv.at[1], me, 1 - core).start()

    loads[6].wait()

    relays = jnp.logical_and(me == 1, core == 1)

    @pl.when(relays)
    def _():
        def forward(i, c):
            place = (slot_of(c), i)
            remote(
                kv.at[m, i], kv.at[place], 4, kv_recv.at[place], c, int(c >= m)
            ).start()

        pl.semaphore_wait(entered, 1)
        for i in range(2):
            wait_bytes(kv.at[m, i], kv_recv.at[m, i])
            forward(i, n - 1)
            forward(i, 1)
        for c in (*range(split, n - 1), *range(2, m)):
            forward(0, c)
            forward(1, c)

    tok = (lax.broadcasted_iota(jnp.int32, (1, rows), 1)) // heads
    q_span = jnp.where(tok < half, order[2 * me], order[2 * me + 1])
    q_pos = q_span * half + tok % half
    q_span = jnp.concatenate([q_span, q_span], axis=1)
    q_pos = jnp.concatenate([q_pos, q_pos], axis=1)
    key_row = lax.broadcasted_iota(jnp.int32, (toks, 1), 0)

    with jax.named_scope("w_pair"):
        wait_bytes(qg.at[1], pair_recv.at[0])
        wait_bytes(stat.at[1], pair_recv.at[1])
    totals = jnp.concatenate([stat[0, 0:1], stat[1, 0:1]], axis=1)
    deltas = jnp.concatenate([stat[0, 1:2], stat[1, 1:2]], axis=1)

    def by_span(a, b):
        return jnp.where(key_row < half, a, b)

    def block(j):
        spans = [order[2 * owners[j] + h] for h in range(2)]
        queries = qg[:, 0].reshape(2 * rows, width)
        grads = qg[:, 1].reshape(2 * rows, width)
        with jax.named_scope(f"w_k{j}"):
            wait_bytes(kv.at[j, 0], kv_recv.at[j, 0])
        with jax.named_scope(f"dv{j}"):
            scores = dot(kv[j, 0], queries, NT)
            if j == 0:
                visible = by_span(*spans) * half + key_row % half <= q_pos
                probs = jnp.exp2(
                    jnp.where(visible, scores * (scale * LOG2E) - totals, -jnp.inf)
                )
            else:
                shifts = [jnp.where(k_span < q_span, totals, jnp.inf) for k_span in spans]
                probs = jnp.exp2(
                    jnp.concatenate(
                        [
                            scores[h * half : (h + 1) * half] * (scale * LOG2E) - shifts[h]
                            for h in range(2)
                        ]
                    )
                )
            yield 1, dot(probs.astype(BF16), grads)
        with jax.named_scope(f"w_v{j}"):
            wait_bytes(kv.at[j, 1], kv_recv.at[j, 1])
        with jax.named_scope(f"dk{j}"):
            grad_probs = dot(kv[j, 1], grads, NT)
            grad_scores = (probs * (grad_probs - deltas)).astype(BF16)
            ds_all[j] = grad_scores
            yield 0, dot(grad_scores, queries) * scale

    for j in range(m):
        at = j + core * (n - 1 - 2 * j)
        for i, grad in block(j):
            send_buf[j, i] = grad.astype(BF16)
            src, dst = send_buf.at[j, i], recv_buf.at[i, at]
            ready = grad_recv.at[i]
            if (j, i) == (0, 0):
                ready = grad_recv.at[2 * core]

                @pl.when(jnp.logical_and(core == 1, me == n - 1))
                def _():
                    remote(src, dst, 5, ready, 0, 0).start()

            remote(src, dst, 3, ready, owners[j], 1).start()

        if j == m - 1:
            middle_sends(me == 1)

    def query_grad(i):
        total = None
        for j in range(m):
            term = dot(ds_all[j, :, i * rows : (i + 1) * rows], kv[j, 0], TN)
            total = term if total is None else total + term
        return total * scale

    pl.when(relays)(lambda: wait_sent(recv_buf.at[:, 0 : n - split + m - 1], 4))

    with jax.named_scope("dq"):
        dq_send[...] = query_grad(1)
        dq_copy = remote(dq_send, dq_recv, 4, pair_recv.at[2], me, 1 - core)
        dq_copy.start()
        own_grad = query_grad(0)
    def sum_near():
        with jax.named_scope("w_near"):
            wait_bytes(recv_buf.at[0, 0 : n - 1], grad_recv.at[0])
        part[...] = sum(recv_buf[0, d].astype(F32) for d in range(n - 1))

    wait_sent(stat.at[0], 2)

    @pl.when(jnp.logical_and(core == 1, me == 0))
    def _():
        sum_near()
        remote(part, part, 2, pair_recv.at[4], me, 0).start()

    with jax.named_scope("w_dq"):
        dq_copy.wait_recv()
    dq_ref[...] = (own_grad + dq_recv[...]).astype(BF16)

    with jax.named_scope("w_sends"):
        wait_sent(qg.at[0], 1)
        wait_sent(send_buf, 3)
        dq_copy.wait_send()

        @pl.when(core == 1)
        def _():
            pl.when(me == 0)(lambda: wait_sent(mine, 0))
            pl.when(me != 0)(lambda: wait_sent(recv_buf.at[:, 0 : n - split], 0))

        @pl.when(jnp.logical_and(core == 0, me != 0))
        def _():
            wait_sent(recv_buf.at[:, 1:split], 0)

        @pl.when(jnp.logical_and(core == 0, me == 0))
        def _():
            wait_sent(recv_buf.at[:, m:split], 0)

    def sum_far():
        with jax.named_scope("w_far"):
            wait_bytes(recv_buf.at[0, n - 1], grad_recv.at[2])
        kv_ref[0] = (part[...] + recv_buf[0, n - 1].astype(F32)).astype(BF16)

    @pl.when(core == 1)
    def _():
        pl.when(me == n - 1)(lambda: wait_sent(send_buf.at[0, 0], 5))
        with jax.named_scope("w_v"):
            wait_bytes(recv_buf.at[1], grad_recv.at[1])
        kv_ref[1] = sum(recv_buf[1, d].astype(F32) for d in range(n)).astype(BF16)
        remote(kv_ref.at[1], kv_ref.at[1], 5, pair_recv.at[3], me, 0).start()
        pl.when(me != 0)(sum_near)
        sum_far()

        @pl.when(me != 0)
        def _():
            remote(kv_ref.at[0], kv_ref.at[0], 5, pair_recv.at[3], me, 0).start()
            wait_sent(kv_ref, 5)

        @pl.when(me == 0)
        def _():
            with jax.named_scope("w_finsend"):
                wait_sent(kv_ref.at[1], 5)
                wait_sent(part, 2)

    @pl.when(core == 0)
    def _():
        @pl.when(me != 0)
        def _():
            with jax.named_scope("w_fin"):
                wait_bytes(kv_ref, pair_recv.at[3])

        @pl.when(me == 0)
        def _():
            with jax.named_scope("w_part"):
                wait_bytes(part, pair_recv.at[4])
            sum_far()
            with jax.named_scope("w_finv"):
                wait_bytes(kv_ref.at[1], pair_recv.at[3])


def store_kernel(dq_ref, kv_ref, dq_hbm, dk_hbm, dv_hbm, sem):
    pairs = ((dq_ref, dq_hbm), (kv_ref.at[0], dk_hbm), (kv_ref.at[1], dv_hbm))
    copies = [pltpu.make_async_copy(a, b, sem.at[i]) for i, (a, b) in enumerate(pairs)]
    for copy in copies:
        copy.start()
    for copy in copies:
        copy.wait()


def body(n, queries, keys, values, out, log_total, d_out, span_order):
    _, toks, heads, width = queries.shape
    rows = toks * heads
    m = n // 2
    flat = lambda x: x.reshape(rows, width)
    anywhere = pl.BlockSpec(memory_space=pltpu.HBM)
    in_vmem = pl.BlockSpec(memory_space=pltpu.VMEM)
    dq, dkv = pl.pallas_call(
        functools.partial(kernel, n, heads),
        out_shape=(
            pltpu.VMEM((rows, width), BF16),
            pltpu.VMEM((2, toks, width), BF16),
        ),
        in_specs=[anywhere] * 7,
        out_specs=(in_vmem,) * 2,
        scratch_shapes=[
            pltpu.VMEM((2, 2, rows, width), BF16),
            pltpu.VMEM((rows, width), BF16),
            pltpu.VMEM((heads, toks), F32),
            pltpu.VMEM((2, toks, width), BF16),
            pltpu.VMEM((m + 1, 2, toks, width), BF16),
            pltpu.VMEM((2, 8, rows), F32),
            pltpu.VMEM((m, toks, 2 * rows), BF16),
            pltpu.VMEM((m, 2, toks, width), BF16),
            pltpu.VMEM((2, n, toks, width), BF16),
            pltpu.VMEM((toks, width), F32),
            pltpu.VMEM((rows, width), F32),
            pltpu.VMEM((rows, width), F32),
            pltpu.SMEM((span_order.shape[1],), jnp.int32),
            pltpu.SemaphoreType.DMA((6,)),
            pltpu.SemaphoreType.DMA((5,)),
            pltpu.SemaphoreType.DMA((m + 1, 2)),
            pltpu.SemaphoreType.DMA((3,)),
            pltpu.SemaphoreType.REGULAR,
        ],
        compiler_params=pltpu.CompilerParams(collective_id=0, has_side_effects=True),
    )(
        flat(queries),
        keys[0],
        values[0],
        flat(out),
        log_total[0],
        flat(d_out),
        span_order[0],
    )
    dq, dk, dv = pl.pallas_call(
        store_kernel,
        out_shape=(
            jax.ShapeDtypeStruct((rows, width), BF16),
            jax.ShapeDtypeStruct((toks, width), BF16),
            jax.ShapeDtypeStruct((toks, width), BF16),
        ),
        in_specs=[in_vmem] * 2,
        out_specs=(anywhere,) * 3,
        scratch_shapes=[pltpu.SemaphoreType.DMA((3,))],
        compiler_params=pltpu.CompilerParams(vmem_limit_bytes=2**20),
    )(dq, dkv)
    return dq.reshape(queries.shape), dk[None], dv[None]


def solution(mesh):
    seq = ("groups", "outer")
    wide = P(seq, "inner", "head", None)
    narrow = P(seq, "inner", None)
    return jax.shard_map(
        functools.partial(body, mesh.shape["inner"]),
        mesh=mesh,
        in_specs=(wide, narrow, narrow, wide, P(seq, "head", "inner"), wide, P(seq, None)),
        out_specs=(wide, narrow, narrow),
        check_vma=False,
    )
```

time: 14.6 us -> 14 us (0.959)
  Pallas kernels: 13.8 us -> 13.2 us
    pallas_call x1, Pallas kernels: 13.1 us -> 12.5 us  [body(): pl.pallas_call(functools.partial(kernel, n, heads), out_shape=(pltpu.VMEM...]
where the time goes in v3:
time: 14 us; the launch traced here: 13.9 us
  Pallas kernels  13.2 us (94%)
  between operations  0.64 us (5%)
    pallas_call x1, Pallas kernels, body(): pl.pallas_call(functools.partial(kernel, n, heads), out_shape=(pltpu.VMEM...  12.5 us
    pallas_call x1, Pallas kernels, body(): pl.pallas_call(store_kernel, out_shape=(jax.ShapeDtypeStruct((rows, width...  0.7 us

profile of v3, /device:TPU:0, one launch (start us, length us, event | category | flops | bytes accessed | tf_op | source)
XLA Modules:
  0.0 13.9 jit_solution(875755865419321969)
XLA Ops:
  0.6 12.5 %shard_map.94 = (bf16[512,128]{1,0:T(8,128)(2,1)S(1)}, bf16[2,128,128]{2,1,0:T(8,128)(2,1)S(1)}) custom-call(bf16[512,128]{1,0:T(8,128)(2,1)} %bitcast.10, bf16[128,128]{1,0:T(8,128)(2,1)} %bitcast.13, bf16[128,128]{1,0:T(8,128)(2,1)} %bitcast.14, bf16[512,128]{1,0:T(8,128)(2,1)} %bitcast.11, f32[4,128]{1,0:T(4,128)} %bitcast.15, bf16[512,128]{1,0:T(8,128)(2,1)} %bitcast.12, ...), custom_call_target="tpu_custom_call" | custom-call | tf_op jit(solution)/shard_map/pallas_call | solution.py:402
  13.2 0.7 %shard_map.95 = (bf16[512,128]{1,0:T(8,128)(2,1)}, bf16[128,128]{1,0:T(8,128)(2,1)}, bf16[128,128]{1,0:T(8,128)(2,1)}) custom-call(bf16[512,128]{1,0:T(8,128)(2,1)S(1)} %get-tuple-element.8.dq_ref, bf16[2,128,128]{2,1,0:T(8,128)(2,1)S(1)} %get-tuple-element.9.kv_ref), custom_call_target="tpu_custom_call" | custom-call | tf_op jit(solution)/shard_map/pallas_call | solution.py:440

commit v4 on v3

--- a/solution.py
+++ b/solution.py
@@ -134,8 +134,8 @@
     def slot_of(d):
         return d if d < m else n - 1 - d
 
-    def kv_send(d):
-        for i in range(2):
+    def kv_send(d, parts=(0, 1)):
+        for i in parts:
             place = (slot_of(d), i)
             remote(
                 mine.at[i], kv.at[place], 0, kv_recv.at[place], chip(d), int(d >= m)
@@ -174,13 +174,14 @@
             for d in range(1, m):
                 kv_send(d)
 
-    def middle_sends(when):
+    def middle_sends(when, parts=(0, 1)):
         @pl.when(jnp.logical_and(core == 0, when))
         def _():
             for d in range(m, split):
-                kv_send(d)
-
-    middle_sends(me != 1)
+                kv_send(d, parts)
+
+    middle_sends(me > 1)
+    middle_sends(me == 0, (0,))
 
     wait_bytes(qg.at[0], sem.at[1])
     remote(qg.at[0], qg.at[1], 1, pair_recv.at[0], me, 1 - core).start()
@@ -271,9 +272,9 @@
             wait_bytes(kv.at[j, 1], kv_recv.at[j, 1])
         with jax.named_scope(f"dk{j}"):
             grad_probs = dot(kv[j, 1], grads, NT)
-            grad_scores = (probs * (grad_probs - deltas)).astype(BF16)
+            grad_scores = (probs * (grad_probs - deltas) * scale).astype(BF16)
             ds_all[j] = grad_scores
-            yield 0, dot(grad_scores, queries) * scale
+            yield 0, dot(grad_scores, queries)
 
     for j in range(m):
         at = j + core * (n - 1 - 2 * j)
@@ -289,16 +290,17 @@
                     remote(src, dst, 5, ready, 0, 0).start()
 
             remote(src, dst, 3, ready, owners[j], 1).start()
-
-        if j == m - 1:
-            middle_sends(me == 1)
+            if (j, i) == (0, 1):
+                middle_sends(me == 0, (1,))
+            if (j, i) == (m - 1, 1):
+                middle_sends(me == 1)
 
     def query_grad(i):
         total = None
         for j in range(m):
             term = dot(ds_all[j, :, i * rows : (i + 1) * rows], kv[j, 0], TN)
             total = term if total is None else total + term
-        return total * scale
+        return total
 
     pl.when(relays)(lambda: wait_sent(recv_buf.at[:, 0 : n - split + m - 1], 4))
 

time: 14 us -> 13.5 us (0.964)
  Pallas kernels: 13.2 us -> 12.7 us
    pallas_call x1, Pallas kernels: 12.5 us -> 12 us  [body(): pl.pallas_call(functools.partial(kernel, n, heads), out_shape=(pltpu.VMEM...]
where the time goes in v4:
time: 13.5 us; the launch traced here: 13.3 us
  Pallas kernels  12.7 us (94%)
  between operations  0.64 us (5%)
    pallas_call x1, Pallas kernels, body(): pl.pallas_call(functools.partial(kernel, n, heads), out_shape=(pltpu.VMEM...  12 us
    pallas_call x1, Pallas kernels, body(): pl.pallas_call(store_kernel, out_shape=(jax.ShapeDtypeStruct((rows, width...  0.7 us

profile of v4, /device:TPU:0, one launch (start us, length us, event | category | flops | bytes accessed | tf_op | source)
XLA Modules:
  0.0 13.3 jit_solution(6810835720046927249)
XLA Ops:
  0.6 12.0 %shard_map.94 = (bf16[512,128]{1,0:T(8,128)(2,1)S(1)}, bf16[2,128,128]{2,1,0:T(8,128)(2,1)S(1)}) custom-call(bf16[512,128]{1,0:T(8,128)(2,1)} %bitcast.10, bf16[128,128]{1,0:T(8,128)(2,1)} %bitcast.13, bf16[128,128]{1,0:T(8,128)(2,1)} %bitcast.14, bf16[512,128]{1,0:T(8,128)(2,1)} %bitcast.11, f32[4,128]{1,0:T(4,128)} %bitcast.15, bf16[512,128]{1,0:T(8,128)(2,1)} %bitcast.12, ...), custom_call_target="tpu_custom_call" | custom-call | tf_op jit(solution)/shard_map/pallas_call | solution.py:404
  12.6 0.7 %shard_map.95 = (bf16[512,128]{1,0:T(8,128)(2,1)}, bf16[128,128]{1,0:T(8,128)(2,1)}, bf16[128,128]{1,0:T(8,128)(2,1)}) custom-call(bf16[512,128]{1,0:T(8,128)(2,1)S(1)} %get-tuple-element.8.dq_ref, bf16[2,128,128]{2,1,0:T(8,128)(2,1)S(1)} %get-tuple-element.9.kv_ref), custom_call_target="tpu_custom_call" | custom-call | tf_op jit(solution)/shard_map/pallas_call | solution.py:442

commit v5 on v4

--- a/solution.py
+++ b/solution.py
@@ -49,6 +49,7 @@
     pair_recv,
     kv_recv,
     grad_recv,
+    entry,
     entered,
 ):
     me = lax.axis_index("inner")
@@ -86,7 +87,7 @@
         for d in reversed(range(split, n)):
             greet(chip(d), 1, chip(d) != 0)
         for d in reversed(range(m, split)):
-            greet(chip(d), 0)
+            greet(chip(d), 0, chip(d) != 0)
         greet(me, 0)
 
     @pl.when(core == 0)
@@ -134,8 +135,8 @@
     def slot_of(d):
         return d if d < m else n - 1 - d
 
-    def kv_send(d, parts=(0, 1)):
-        for i in parts:
+    def kv_send(d):
+        for i in range(2):
             place = (slot_of(d), i)
             remote(
                 mine.at[i], kv.at[place], 0, kv_recv.at[place], chip(d), int(d >= m)
@@ -144,17 +145,23 @@
     wait_bytes(mine, sem.at[0])
     sent = jnp.where(
         me == 0,
-        jnp.where(core == 1, 1, split - m),
+        core,
         jnp.where(core == 1, n - split, split - 1),
     )
     pl.semaphore_wait(barrier, 1 + sent)
 
+    pieces = [
+        ((0, pl.ds(0, half)), entry.at[0]),
+        ((0, pl.ds(half, half)), entry.at[1]),
+        ((1,), entry.at[2]),
+    ]
+
     @pl.when(me == 0)
     def _():
         @pl.when(core == 1)
         def _():
-            for i in range(2):
-                remote(mine.at[i], kv.at[m, i], 0, kv_recv.at[m, i], 1, 1).start()
+            for piece, ready in pieces:
+                remote(mine.at[piece], kv.at[(m, *piece)], 0, ready, 1, 1).start()
 
     @pl.when(me != 0)
     def _():
@@ -174,14 +181,13 @@
             for d in range(1, m):
                 kv_send(d)
 
-    def middle_sends(when, parts=(0, 1)):
+    def middle_sends(when):
         @pl.when(jnp.logical_and(core == 0, when))
         def _():
             for d in range(m, split):
-                kv_send(d, parts)
+                kv_send(d)
 
     middle_sends(me > 1)
-    middle_sends(me == 0, (0,))
 
     wait_bytes(qg.at[0], sem.at[1])
     remote(qg.at[0], qg.at[1], 1, pair_recv.at[0], me, 1 - core).start()
@@ -213,20 +219,23 @@
 
     @pl.when(relays)
     def _():
-        def forward(i, c):
-            place = (slot_of(c), i)
+        def forward(piece, c):
+            place = (slot_of(c), *piece)
             remote(
-                kv.at[m, i], kv.at[place], 4, kv_recv.at[place], c, int(c >= m)
+                kv.at[(m, *piece)], kv.at[place], 4, kv_recv.at[place[:2]], c, int(c >= m)
             ).start()
 
         pl.semaphore_wait(entered, 1)
-        for i in range(2):
-            wait_bytes(kv.at[m, i], kv_recv.at[m, i])
-            forward(i, n - 1)
-            forward(i, 1)
-        for c in (*range(split, n - 1), *range(2, m)):
-            forward(0, c)
-            forward(1, c)
+        rest = [*range(m, n - 1), 1, *range(2, m)]
+        for piece, ready in pieces[:2]:
+            wait_bytes(kv.at[(m, *piece)], ready)
+            forward(piece, n - 1)
+        for c in rest:
+            forward((0,), c)
+        piece, ready = pieces[2]
+        wait_bytes(kv.at[(m, *piece)], ready)
+        for c in (*rest, n - 1):
+            forward(piece, c)
 
     tok = (lax.broadcasted_iota(jnp.int32, (1, rows), 1)) // heads
     q_span = jnp.where(tok < half, order[2 * me], order[2 * me + 1])
@@ -276,22 +285,25 @@
             ds_all[j] = grad_scores
             yield 0, dot(grad_scores, queries)
 
+    last = jnp.logical_and(core == 1, me == n - 1)
+    held = jnp.logical_and(core == 0, me == n - 1)
+
+    def grad_copy(j, i, head=1):
+        spare = i == 0
+        ready = grad_recv.at[jnp.where(last, 2, 0)] if spare else grad_recv.at[1]
+        return remote(
+            send_buf.at[j, i], recv_buf.at[i, me], 3 if head else 5, ready, owners[j], head
+        )
+
     for j in range(m):
-        at = j + core * (n - 1 - 2 * j)
         for i, grad in block(j):
             send_buf[j, i] = grad.astype(BF16)
-            src, dst = send_buf.at[j, i], recv_buf.at[i, at]
-            ready = grad_recv.at[i]
-            if (j, i) == (0, 0):
-                ready = grad_recv.at[2 * core]
-
-                @pl.when(jnp.logical_and(core == 1, me == n - 1))
-                def _():
-                    remote(src, dst, 5, ready, 0, 0).start()
-
-            remote(src, dst, 3, ready, owners[j], 1).start()
-            if (j, i) == (0, 1):
-                middle_sends(me == 0, (1,))
+            if i == 0:
+                pl.when(last)(lambda: grad_copy(j, i, 0).start())
+            if j:
+                pl.when(jnp.logical_not(held))(lambda: grad_copy(j, i).start())
+            else:
+                grad_copy(j, i).start()
             if (j, i) == (m - 1, 1):
                 middle_sends(me == 1)
 
@@ -302,23 +314,32 @@
             total = term if total is None else total + term
         return total
 
-    pl.when(relays)(lambda: wait_sent(recv_buf.at[:, 0 : n - split + m - 1], 4))
+    pl.when(relays)(lambda: wait_sent(recv_buf.at[:, 0 : n - 1], 4))
 
     with jax.named_scope("dq"):
         dq_send[...] = query_grad(1)
         dq_copy = remote(dq_send, dq_recv, 4, pair_recv.at[2], me, 1 - core)
         dq_copy.start()
         own_grad = query_grad(0)
-    def sum_near():
+
+    @pl.when(held)
+    def _():
+        for j in range(1, m):
+            for i in (1, 0):
+                grad_copy(j, i).start()
+
+    lower = me < m
+
+    def sum_near(count):
         with jax.named_scope("w_near"):
-            wait_bytes(recv_buf.at[0, 0 : n - 1], grad_recv.at[0])
-        part[...] = sum(recv_buf[0, d].astype(F32) for d in range(n - 1))
+            wait_bytes(recv_buf.at[0, 0:count], grad_recv.at[0])
+        return sum(recv_buf[0, c].astype(F32) for c in range(count))
 
     wait_sent(stat.at[0], 2)
 
-    @pl.when(jnp.logical_and(core == 1, me == 0))
-    def _():
-        sum_near()
+    @pl.when(jnp.logical_and(core == 1, lower))
+    def _():
+        part[...] = sum_near(n - 1)
         remote(part, part, 2, pair_recv.at[4], me, 0).start()
 
     with jax.named_scope("w_dq"):
@@ -339,10 +360,6 @@
         def _():
             wait_sent(recv_buf.at[:, 1:split], 0)
 
-        @pl.when(jnp.logical_and(core == 0, me == 0))
-        def _():
-            wait_sent(recv_buf.at[:, m:split], 0)
-
     def sum_far():
         with jax.named_scope("w_far"):
             wait_bytes(recv_buf.at[0, n - 1], grad_recv.at[2])
@@ -350,33 +367,33 @@
 
     @pl.when(core == 1)
     def _():
-        pl.when(me == n - 1)(lambda: wait_sent(send_buf.at[0, 0], 5))
+        pl.when(last)(lambda: wait_sent(recv_buf.at[0, 0:m], 5))
         with jax.named_scope("w_v"):
             wait_bytes(recv_buf.at[1], grad_recv.at[1])
-        kv_ref[1] = sum(recv_buf[1, d].astype(F32) for d in range(n)).astype(BF16)
+        kv_ref[1] = sum(recv_buf[1, c].astype(F32) for c in range(n)).astype(BF16)
         remote(kv_ref.at[1], kv_ref.at[1], 5, pair_recv.at[3], me, 0).start()
-        pl.when(me != 0)(sum_near)
-        sum_far()
-
-        @pl.when(me != 0)
-        def _():
+
+        @pl.when(jnp.logical_not(lower))
+        def _():
+            kv_ref[0] = sum_near(n).astype(BF16)
             remote(kv_ref.at[0], kv_ref.at[0], 5, pair_recv.at[3], me, 0).start()
             wait_sent(kv_ref, 5)
 
-        @pl.when(me == 0)
-        def _():
+        @pl.when(lower)
+        def _():
+            sum_far()
             with jax.named_scope("w_finsend"):
                 wait_sent(kv_ref.at[1], 5)
                 wait_sent(part, 2)
 
     @pl.when(core == 0)
     def _():
-        @pl.when(me != 0)
+        @pl.when(jnp.logical_not(lower))
         def _():
             with jax.named_scope("w_fin"):
                 wait_bytes(kv_ref, pair_recv.at[3])
 
-        @pl.when(me == 0)
+        @pl.when(lower)
         def _():
             with jax.named_scope("w_part"):
                 wait_bytes(part, pair_recv.at[4])
@@ -425,7 +442,8 @@
             pltpu.SMEM((span_order.shape[1],), jnp.int32),
             pltpu.SemaphoreType.DMA((6,)),
             pltpu.SemaphoreType.DMA((5,)),
-            pltpu.SemaphoreType.DMA((m + 1, 2)),
+            pltpu.SemaphoreType.DMA((m, 2)),
+            pltpu.SemaphoreType.DMA((3,)),
             pltpu.SemaphoreType.DMA((3,)),
             pltpu.SemaphoreType.REGULAR,
         ],

time: 13.5 us -> 13.4 us (level)
  no operation moved by 1% of the time
where the time goes in v5:
time: 13.4 us; the launch traced here: 13.2 us
  Pallas kernels  12.6 us (94%)
  between operations  0.64 us (5%)
    pallas_call x1, Pallas kernels, body(): pl.pallas_call(functools.partial(kernel, n, heads), out_shape=(pltpu.VMEM...  11.9 us
    pallas_call x1, Pallas kernels, body(): pl.pallas_call(store_kernel, out_shape=(jax.ShapeDtypeStruct((rows, width...  0.7 us

profile of v5, /device:TPU:0, one launch (start us, length us, event | category | flops | bytes accessed | tf_op | source)
XLA Modules:
  0.0 13.2 jit_solution(54917014421151527)
XLA Ops:
  0.6 11.9 %shard_map.94 = (bf16[512,128]{1,0:T(8,128)(2,1)S(1)}, bf16[2,128,128]{2,1,0:T(8,128)(2,1)S(1)}) custom-call(bf16[512,128]{1,0:T(8,128)(2,1)} %bitcast.10, bf16[128,128]{1,0:T(8,128)(2,1)} %bitcast.13, bf16[128,128]{1,0:T(8,128)(2,1)} %bitcast.14, bf16[512,128]{1,0:T(8,128)(2,1)} %bitcast.11, f32[4,128]{1,0:T(4,128)} %bitcast.15, bf16[512,128]{1,0:T(8,128)(2,1)} %bitcast.12, ...), custom_call_target="tpu_custom_call" | custom-call | tf_op jit(solution)/shard_map/pallas_call | solution.py:421
  12.6 0.7 %shard_map.95 = (bf16[512,128]{1,0:T(8,128)(2,1)}, bf16[128,128]{1,0:T(8,128)(2,1)}, bf16[128,128]{1,0:T(8,128)(2,1)}) custom-call(bf16[512,128]{1,0:T(8,128)(2,1)S(1)} %get-tuple-element.8.dq_ref, bf16[2,128,128]{2,1,0:T(8,128)(2,1)S(1)} %get-tuple-element.9.kv_ref), custom_call_target="tpu_custom_call" | custom-call | tf_op jit(solution)/shard_map/pallas_call | solution.py:460

commit v6 on v5

--- a/solution.py
+++ b/solution.py
@@ -30,8 +30,7 @@
     l_hbm,
     g_hbm,
     order_hbm,
-    dq_ref,
-    kv_ref,
+    out_ref,
     qg,
     os_,
     ls,
@@ -59,6 +58,8 @@
     toks, width = kv.shape[2], kv.shape[3]
     half = toks // 2
     rows = qg.shape[2]
+    dq_ref, kv_out = out_ref.at[pl.ds(0, rows)], out_ref.at[pl.ds(rows, 2 * toks)]
+    grad_out = [out_ref.at[pl.ds(rows + i * toks, toks)] for i in range(2)]
     scale = 1.0 / math.sqrt(width)
     partner = {"head": 1 - core}
 
@@ -178,8 +179,10 @@
                     entered, inc=1, device_id={"inner": me, "head": 1}, device_id_type=MESH
                 )
 
-            for d in range(1, m):
-                kv_send(d)
+            @pl.when(me == 1)
+            def _():
+                for d in range(1, m):
+                    kv_send(d)
 
     def middle_sends(when):
         @pl.when(jnp.logical_and(core == 0, when))
@@ -188,6 +191,11 @@
                 kv_send(d)
 
     middle_sends(me > 1)
+
+    @pl.when(jnp.logical_and(core == 0, me > 1))
+    def _():
+        for d in range(1, m):
+            kv_send(d)
 
     wait_bytes(qg.at[0], sem.at[1])
     remote(qg.at[0], qg.at[1], 1, pair_recv.at[0], me, 1 - core).start()
@@ -337,6 +345,14 @@
 
     wait_sent(stat.at[0], 2)
 
+    def finish_values():
+        with jax.named_scope("w_v"):
+            wait_bytes(recv_buf.at[1], grad_recv.at[1])
+        grad_out[1][...] = sum(recv_buf[1, c].astype(F32) for c in range(n)).astype(BF16)
+        remote(grad_out[1], grad_out[1], 5, pair_recv.at[3], me, 0).start()
+
+    pl.when(jnp.logical_and(core == 1, me == 0))(finish_values)
+
     @pl.when(jnp.logical_and(core == 1, lower))
     def _():
         part[...] = sum_near(n - 1)
@@ -363,27 +379,24 @@
     def sum_far():
         with jax.named_scope("w_far"):
             wait_bytes(recv_buf.at[0, n - 1], grad_recv.at[2])
-        kv_ref[0] = (part[...] + recv_buf[0, n - 1].astype(F32)).astype(BF16)
+        grad_out[0][...] = (part[...] + recv_buf[0, n - 1].astype(F32)).astype(BF16)
 
     @pl.when(core == 1)
     def _():
         pl.when(last)(lambda: wait_sent(recv_buf.at[0, 0:m], 5))
-        with jax.named_scope("w_v"):
-            wait_bytes(recv_buf.at[1], grad_recv.at[1])
-        kv_ref[1] = sum(recv_buf[1, c].astype(F32) for c in range(n)).astype(BF16)
-        remote(kv_ref.at[1], kv_ref.at[1], 5, pair_recv.at[3], me, 0).start()
+        pl.when(me != 0)(finish_values)
 
         @pl.when(jnp.logical_not(lower))
         def _():
-            kv_ref[0] = sum_near(n).astype(BF16)
-            remote(kv_ref.at[0], kv_ref.at[0], 5, pair_recv.at[3], me, 0).start()
-            wait_sent(kv_ref, 5)
+            grad_out[0][...] = sum_near(n).astype(BF16)
+            remote(grad_out[0], grad_out[0], 5, pair_recv.at[3], me, 0).start()
+            wait_sent(kv_out, 5)
 
         @pl.when(lower)
         def _():
             sum_far()
             with jax.named_scope("w_finsend"):
-                wait_sent(kv_ref.at[1], 5)
+                wait_sent(grad_out[1], 5)
                 wait_sent(part, 2)
 
     @pl.when(core == 0)
@@ -391,7 +404,7 @@
         @pl.when(jnp.logical_not(lower))
         def _():
             with jax.named_scope("w_fin"):
-                wait_bytes(kv_ref, pair_recv.at[3])
+                wait_bytes(kv_out, pair_recv.at[3])
 
         @pl.when(lower)
         def _():
@@ -399,16 +412,16 @@
                 wait_bytes(part, pair_recv.at[4])
             sum_far()
             with jax.named_scope("w_finv"):
-                wait_bytes(kv_ref.at[1], pair_recv.at[3])
-
-
-def store_kernel(dq_ref, kv_ref, dq_hbm, dk_hbm, dv_hbm, sem):
-    pairs = ((dq_ref, dq_hbm), (kv_ref.at[0], dk_hbm), (kv_ref.at[1], dv_hbm))
-    copies = [pltpu.make_async_copy(a, b, sem.at[i]) for i, (a, b) in enumerate(pairs)]
-    for copy in copies:
-        copy.start()
-    for copy in copies:
-        copy.wait()
+                wait_bytes(grad_out[1], pair_recv.at[3])
+
+
+def store_kernel(out_ref, dq_hbm, dk_hbm, dv_hbm, sem):
+    start = 0
+    for dst in (dq_hbm, dk_hbm, dv_hbm):
+        span = pl.ds(start, dst.shape[0])
+        pltpu.make_async_copy(out_ref.at[span], dst, sem).start()
+        start += dst.shape[0]
+    pltpu.make_async_copy(out_ref, out_ref, sem).wait()
 
 
 def body(n, queries, keys, values, out, log_total, d_out, span_order):
@@ -418,14 +431,11 @@
     flat = lambda x: x.reshape(rows, width)
     anywhere = pl.BlockSpec(memory_space=pltpu.HBM)
     in_vmem = pl.BlockSpec(memory_space=pltpu.VMEM)
-    dq, dkv = pl.pallas_call(
+    grads = pl.pallas_call(
         functools.partial(kernel, n, heads),
-        out_shape=(
-            pltpu.VMEM((rows, width), BF16),
-            pltpu.VMEM((2, toks, width), BF16),
-        ),
+        out_shape=pltpu.VMEM((rows + 2 * toks, width), BF16),
         in_specs=[anywhere] * 7,
-        out_specs=(in_vmem,) * 2,
+        out_specs=in_vmem,
         scratch_shapes=[
             pltpu.VMEM((2, 2, rows, width), BF16),
             pltpu.VMEM((rows, width), BF16),
@@ -464,11 +474,11 @@
             jax.ShapeDtypeStruct((toks, width), BF16),
             jax.ShapeDtypeStruct((toks, width), BF16),
         ),
-        in_specs=[in_vmem] * 2,
+        in_specs=[in_vmem],
         out_specs=(anywhere,) * 3,
-        scratch_shapes=[pltpu.SemaphoreType.DMA((3,))],
+        scratch_shapes=[pltpu.SemaphoreType.DMA],
         compiler_params=pltpu.CompilerParams(vmem_limit_bytes=2**20),
-    )(dq, dkv)
+    )(grads)
     return dq.reshape(queries.shape), dk[None], dv[None]
 
 

time: 13.4 us -> 13.3 us (level)
  no operation moved by 1% of the time
where the time goes in v6:
time: 13.3 us; the launch traced here: 13.2 us
  Pallas kernels  12.5 us (94%)
  between operations  0.64 us (5%)
    pallas_call x1, Pallas kernels, body(): pl.pallas_call(functools.partial(kernel, n, heads), out_shape=pltpu.VMEM(...  11.9 us
    pallas_call x1, Pallas kernels, body(): pl.pallas_call(store_kernel, out_shape=(jax.ShapeDtypeStruct((rows, width...  0.68 us

profile of v6, /device:TPU:0, one launch (start us, length us, event | category | flops | bytes accessed | tf_op | source)
XLA Modules:
  0.0 13.2 jit_solution(6093394928512445610)
XLA Ops:
  0.6 11.9 %shard_map.94.out_ref = bf16[768,128]{1,0:T(8,128)(2,1)S(1)} custom-call(bf16[512,128]{1,0:T(8,128)(2,1)} %bitcast.10, bf16[128,128]{1,0:T(8,128)(2,1)} %bitcast.13, bf16[128,128]{1,0:T(8,128)(2,1)} %bitcast.14, bf16[512,128]{1,0:T(8,128)(2,1)} %bitcast.11, f32[4,128]{1,0:T(4,128)} %bitcast.15, bf16[512,128]{1,0:T(8,128)(2,1)} %bitcast.12, s32[8]{0:T(128)} %bitcast.16), custom_call_target="tpu_custom_call" | custom-call | tf_op jit(solution)/shard_map/pallas_call | solution.py:434
  12.5 0.7 %shard_map.95 = (bf16[512,128]{1,0:T(8,128)(2,1)}, bf16[128,128]{1,0:T(8,128)(2,1)}, bf16[128,128]{1,0:T(8,128)(2,1)}) custom-call(bf16[768,128]{1,0:T(8,128)(2,1)S(1)} %shard_map.94.out_ref), custom_call_target="tpu_custom_call" | custom-call | tf_op jit(solution)/shard_map/pallas_call | solution.py:470

commit v7 on v6

--- a/solution.py
+++ b/solution.py
@@ -233,16 +233,18 @@
                 kv.at[(m, *piece)], kv.at[place], 4, kv_recv.at[place[:2]], c, int(c >= m)
             ).start()
 
-        pl.semaphore_wait(entered, 1)
-        rest = [*range(m, n - 1), 1, *range(2, m)]
+        greeted = [c for c in range(m, n - 1) if c ^ 1 >= split]
+        rest = [c for c in range(1, n - 1) if c not in greeted]
         for piece, ready in pieces[:2]:
             wait_bytes(kv.at[(m, *piece)], ready)
-            forward(piece, n - 1)
-        for c in rest:
+            for c in greeted:
+                forward(piece, c)
+        pl.semaphore_wait(entered, 1)
+        for c in (n - 1, *rest):
             forward((0,), c)
         piece, ready = pieces[2]
         wait_bytes(kv.at[(m, *piece)], ready)
-        for c in (*rest, n - 1):
+        for c in (*greeted, *rest, n - 1):
             forward(piece, c)
 
     tok = (lax.broadcasted_iota(jnp.int32, (1, rows), 1)) // heads
@@ -351,12 +353,12 @@
         grad_out[1][...] = sum(recv_buf[1, c].astype(F32) for c in range(n)).astype(BF16)
         remote(grad_out[1], grad_out[1], 5, pair_recv.at[3], me, 0).start()
 
-    pl.when(jnp.logical_and(core == 1, me == 0))(finish_values)
-
     @pl.when(jnp.logical_and(core == 1, lower))
     def _():
         part[...] = sum_near(n - 1)
         remote(part, part, 2, pair_recv.at[4], me, 0).start()
+
+    pl.when(jnp.logical_and(core == 1, me == 0))(finish_values)
 
     with jax.named_scope("w_dq"):
         dq_copy.wait_recv()

time: 13.3 us -> 13.2 us (level)
  no operation moved by 1% of the time
where the time goes in v7:
time: 13.2 us; the launch traced here: 13.1 us
  Pallas kernels  12.4 us (94%)
  between operations  0.64 us (5%)
    pallas_call x1, Pallas kernels, body(): pl.pallas_call(functools.partial(kernel, n, heads), out_shape=pltpu.VMEM(...  11.7 us
    pallas_call x1, Pallas kernels, body(): pl.pallas_call(store_kernel, out_shape=(jax.ShapeDtypeStruct((rows, width...  0.68 us

profile of v7, /device:TPU:0, one launch (start us, length us, event | category | flops | bytes accessed | tf_op | source)
XLA Modules:
  0.0 13.1 jit_solution(996564612398503500)
XLA Ops:
  0.6 11.7 %shard_map.94.out_ref = bf16[768,128]{1,0:T(8,128)(2,1)S(1)} custom-call(bf16[512,128]{1,0:T(8,128)(2,1)} %bitcast.10, bf16[128,128]{1,0:T(8,128)(2,1)} %bitcast.13, bf16[128,128]{1,0:T(8,128)(2,1)} %bitcast.14, bf16[512,128]{1,0:T(8,128)(2,1)} %bitcast.11, f32[4,128]{1,0:T(4,128)} %bitcast.15, bf16[512,128]{1,0:T(8,128)(2,1)} %bitcast.12, s32[8]{0:T(128)} %bitcast.16), custom_call_target="tpu_custom_call" | custom-call | tf_op jit(solution)/shard_map/pallas_call | solution.py:436
  12.4 0.7 %shard_map.95 = (bf16[512,128]{1,0:T(8,128)(2,1)}, bf16[128,128]{1,0:T(8,128)(2,1)}, bf16[128,128]{1,0:T(8,128)(2,1)}) custom-call(bf16[768,128]{1,0:T(8,128)(2,1)S(1)} %shard_map.94.out_ref), custom_call_target="tpu_custom_call" | custom-call | tf_op jit(solution)/shard_map/pallas_call | solution.py:472

commit v8 on v7

--- a/solution.py
+++ b/solution.py
@@ -314,7 +314,7 @@
                 pl.when(jnp.logical_not(held))(lambda: grad_copy(j, i).start())
             else:
                 grad_copy(j, i).start()
-            if (j, i) == (m - 1, 1):
+            if (j, i) == (0, 0):
                 middle_sends(me == 1)
 
     def query_grad(i):

time: 13.2 us -> 13.2 us (level)
  no operation moved by 1% of the time
where the time goes in v8:
time: 13.2 us; the launch traced here: 13.1 us
  Pallas kernels  12.4 us (94%)
  between operations  0.64 us (5%)
    pallas_call x1, Pallas kernels, body(): pl.pallas_call(functools.partial(kernel, n, heads), out_shape=pltpu.VMEM(...  11.7 us
    pallas_call x1, Pallas kernels, body(): pl.pallas_call(store_kernel, out_shape=(jax.ShapeDtypeStruct((rows, width...  0.68 us

profile of v8, /device:TPU:0, one launch (start us, length us, event | category | flops | bytes accessed | tf_op | source)
XLA Modules:
  0.0 13.1 jit_solution(4726208314526764461)
XLA Ops:
  0.6 11.7 %shard_map.94.out_ref = bf16[768,128]{1,0:T(8,128)(2,1)S(1)} custom-call(bf16[512,128]{1,0:T(8,128)(2,1)} %bitcast.10, bf16[128,128]{1,0:T(8,128)(2,1)} %bitcast.13, bf16[128,128]{1,0:T(8,128)(2,1)} %bitcast.14, bf16[512,128]{1,0:T(8,128)(2,1)} %bitcast.11, f32[4,128]{1,0:T(4,128)} %bitcast.15, bf16[512,128]{1,0:T(8,128)(2,1)} %bitcast.12, s32[8]{0:T(128)} %bitcast.16), custom_call_target="tpu_custom_call" | custom-call | tf_op jit(solution)/shard_map/pallas_call | solution.py:436
  12.4 0.7 %shard_map.95 = (bf16[512,128]{1,0:T(8,128)(2,1)}, bf16[128,128]{1,0:T(8,128)(2,1)}, bf16[128,128]{1,0:T(8,128)(2,1)}) custom-call(bf16[768,128]{1,0:T(8,128)(2,1)S(1)} %shard_map.94.out_ref), custom_call_target="tpu_custom_call" | custom-call | tf_op jit(solution)/shard_map/pallas_call | solution.py:472

commit v9 on v8

--- a/solution.py
+++ b/solution.py
@@ -286,30 +286,40 @@
                         ]
                     )
                 )
-            yield 1, dot(probs.astype(BF16), grads)
+            scaled = probs * scale
+            yield 1, slice(0, toks), dot(probs.astype(BF16), grads)
         with jax.named_scope(f"w_v{j}"):
             wait_bytes(kv.at[j, 1], kv_recv.at[j, 1])
         with jax.named_scope(f"dk{j}"):
             grad_probs = dot(kv[j, 1], grads, NT)
-            grad_scores = (probs * (grad_probs - deltas) * scale).astype(BF16)
+            grad_scores = (scaled * (grad_probs - deltas)).astype(BF16)
             ds_all[j] = grad_scores
-            yield 0, dot(grad_scores, queries)
+            for span in (slice(0, half), slice(half, toks)):
+                yield 0, span, dot(grad_scores[span], queries)
 
     last = jnp.logical_and(core == 1, me == n - 1)
     held = jnp.logical_and(core == 0, me == n - 1)
 
-    def grad_copy(j, i, head=1):
+    def grad_copy(j, i, head=1, span=slice(0, None)):
+        rows_of = pl.ds(span.start, (span.stop or toks) - span.start)
         spare = i == 0
         ready = grad_recv.at[jnp.where(last, 2, 0)] if spare else grad_recv.at[1]
         return remote(
-            send_buf.at[j, i], recv_buf.at[i, me], 3 if head else 5, ready, owners[j], head
+            send_buf.at[j, i, rows_of],
+            recv_buf.at[i, me, rows_of],
+            3 if head else 5,
+            ready,
+            owners[j],
+            head,
         )
 
     for j in range(m):
-        for i, grad in block(j):
-            send_buf[j, i] = grad.astype(BF16)
+        for i, span, grad in block(j):
+            send_buf[j, i, span] = grad.astype(BF16)
             if i == 0:
-                pl.when(last)(lambda: grad_copy(j, i, 0).start())
+                pl.when(last)(lambda: grad_copy(j, i, 0, span).start())
+                if span.stop < toks:
+                    continue
             if j:
                 pl.when(jnp.logical_not(held))(lambda: grad_copy(j, i).start())
             else:

time: 13.2 us -> 13.2 us (level)
  no operation moved by 1% of the time
where the time goes in v9:
time: 13.2 us; the launch traced here: 13 us
  Pallas kernels  12.4 us (94%)
  between operations  0.64 us (5%)
    pallas_call x1, Pallas kernels, body(): pl.pallas_call(functools.partial(kernel, n, heads), out_shape=pltpu.VMEM(...  11.7 us
    pallas_call x1, Pallas kernels, body(): pl.pallas_call(store_kernel, out_shape=(jax.ShapeDtypeStruct((rows, width...  0.68 us

profile of v9, /device:TPU:0, one launch (start us, length us, event | category | flops | bytes accessed | tf_op | source)
XLA Modules:
  0.0 13.0 jit_solution(13736139539699923389)
XLA Ops:
  0.6 11.7 %shard_map.94.out_ref = bf16[768,128]{1,0:T(8,128)(2,1)S(1)} custom-call(bf16[512,128]{1,0:T(8,128)(2,1)} %bitcast.10, bf16[128,128]{1,0:T(8,128)(2,1)} %bitcast.13, bf16[128,128]{1,0:T(8,128)(2,1)} %bitcast.14, bf16[512,128]{1,0:T(8,128)(2,1)} %bitcast.11, f32[4,128]{1,0:T(4,128)} %bitcast.15, bf16[512,128]{1,0:T(8,128)(2,1)} %bitcast.12, s32[8]{0:T(128)} %bitcast.16), custom_call_target="tpu_custom_call" | custom-call | tf_op jit(solution)/shard_map/pallas_call | solution.py:446
  12.4 0.7 %shard_map.95 = (bf16[512,128]{1,0:T(8,128)(2,1)}, bf16[128,128]{1,0:T(8,128)(2,1)}, bf16[128,128]{1,0:T(8,128)(2,1)}) custom-call(bf16[768,128]{1,0:T(8,128)(2,1)S(1)} %shard_map.94.out_ref), custom_call_target="tpu_custom_call" | custom-call | tf_op jit(solution)/shard_map/pallas_call | solution.py:482
